TPU v7x, 32 devices: a whole 2x2x4 slice. The times are simulated.
32 devices in a mesh: dp: 16 (over z, y, x), mp: 2 (over core).
Axes of the slice: x: 2, y: 2, z: 4, core: 2. Of those that a mesh axis runs over, the one named last changes fastest.
Arguments:
- tokens: bfloat16 [192, 196, 512], P('dp'), may hold values from -6 to 6
- cotangent: float32 [192, 196, 512], P('dp'), may hold values from -6 to 6
- image_count: int32 [16], P('dp'), may hold values from 1 to 12, as said below
- rel_index: int32 [49, 49], replicated, may hold values from 0 to 168, as said below
- w_qkv: float32 [2, 512, 3, 512], P(None, 'dp', None, 'mp'), may hold values from -0.25 to 0.25
- w_proj: float32 [2, 512, 512], P(None, 'mp', 'dp'), may hold values from -0.5 to 0.5
- w_fc_one: float32 [2, 512, 2048], P(None, 'dp', 'mp'), may hold values from -0.25 to 0.25
- w_fc_two: float32 [2, 2048, 512], P(None, 'mp', 'dp'), may hold values from -0.125 to 0.125
- qv_bias: float32 [2, 2, 512], P(None, None, 'mp'), may hold values from -3 to 3
- fc_one_bias: float32 [2, 2048], P(None, 'mp'), may hold values from -3 to 3
- rel_table: float32 [2, 169, 16], P(None, None, 'mp'), may hold values from -4 to 4
- norm_vec: float32 [2, 6, 512], replicated, may hold values from 0.1 to 1.9
- m_qkv: float32 [2, 512, 3, 512], P(None, 'dp', None, 'mp'), may hold values from -40 to 40
- m_proj: float32 [2, 512, 512], P(None, 'mp', 'dp'), may hold values from -40 to 40
- m_fc_one: float32 [2, 512, 2048], P(None, 'dp', 'mp'), may hold values from -40 to 40
- m_fc_two: float32 [2, 2048, 512], P(None, 'mp', 'dp'), may hold values from -40 to 40
- m_qv_bias: float32 [2, 2, 512], P(None, None, 'mp'), may hold values from -40 to 40
- m_fc_one_bias: float32 [2, 2048], P(None, 'mp'), may hold values from -40 to 40
- m_rel_table: float32 [2, 169, 16], P(None, None, 'mp'), may hold values from -40 to 40
- m_norm_vec: float32 [2, 6, 512], replicated, may hold values from -40 to 40
- v_qkv: float32 [2, 512, 3, 512], P(None, 'dp', None, 'mp'), may hold values from 3.7632 to 37.632
- v_proj: float32 [2, 512, 512], P(None, 'mp', 'dp'), may hold values from 3.7632 to 37.632
- v_fc_one: float32 [2, 512, 2048], P(None, 'dp', 'mp'), may hold values from 3.7632 to 37.632
- v_fc_two: float32 [2, 2048, 512], P(None, 'mp', 'dp'), may hold values from 3.7632 to 37.632
- v_qv_bias: float32 [2, 2, 512], P(None, None, 'mp'), may hold values from 3.7632 to 37.632
- v_fc_one_bias: float32 [2, 2048], P(None, 'mp'), may hold values from 3.7632 to 37.632
- v_rel_table: float32 [2, 169, 16], P(None, None, 'mp'), may hold values from 3.7632 to 37.632
- v_norm_vec: float32 [2, 6, 512], replicated, may hold values from 3.7632 to 37.632
Outputs:
- out: float32 [192, 196, 512], P('dp')
- x_grad: float32 [192, 196, 512], P('dp')
- new_w_qkv: float32 [2, 512, 3, 512], P(None, 'dp', None, 'mp')
- new_w_proj: float32 [2, 512, 512], P(None, 'mp', 'dp')
- new_w_fc_one: float32 [2, 512, 2048], P(None, 'dp', 'mp')
- new_w_fc_two: float32 [2, 2048, 512], P(None, 'mp', 'dp')
- new_qv_bias: float32 [2, 2, 512], P(None, None, 'mp')
- new_fc_one_bias: float32 [2, 2048], P(None, 'mp')
- new_rel_table: float32 [2, 169, 16], P(None, None, 'mp')
- new_norm_vec: float32 [2, 6, 512], replicated
- new_m_qkv: float32 [2, 512, 3, 512], P(None, 'dp', None, 'mp')
- new_m_proj: float32 [2, 512, 512], P(None, 'mp', 'dp')
- new_m_fc_one: float32 [2, 512, 2048], P(None, 'dp', 'mp')
- new_m_fc_two: float32 [2, 2048, 512], P(None, 'mp', 'dp')
- new_m_qv_bias: float32 [2, 2, 512], P(None, None, 'mp')
- new_m_fc_one_bias: float32 [2, 2048], P(None, 'mp')
- new_m_rel_table: float32 [2, 169, 16], P(None, None, 'mp')
- new_m_norm_vec: float32 [2, 6, 512], replicated
- new_v_qkv: float32 [2, 512, 3, 512], P(None, 'dp', None, 'mp')
- new_v_proj: float32 [2, 512, 512], P(None, 'mp', 'dp')
- new_v_fc_one: float32 [2, 512, 2048], P(None, 'dp', 'mp')
- new_v_fc_two: float32 [2, 2048, 512], P(None, 'mp', 'dp')
- new_v_qv_bias: float32 [2, 2, 512], P(None, None, 'mp')
- new_v_fc_one_bias: float32 [2, 2048], P(None, 'mp')
- new_v_rel_table: float32 [2, 169, 16], P(None, None, 'mp')
- new_v_norm_vec: float32 [2, 6, 512], replicated
Inputs may be any that keep to these rules, and one draw needn't show every extreme that they name: `image_count`: slots below a device's count hold live images; some index of dp holds 12. `rel_index`: pairs of window positions with the same relative offset share one entry; distinct offsets have distinct entries.
All inputs are finite; a program needn't handle non-finite values.
Results may differ from a plain program's by a relative error of at most 0.023.
Values may be sent and summed in bfloat16 or wider, within the bound.
A program may use at most 320 MiB of HBM per device.

v0:
```python
import jax
import jax.numpy as jnp
from jax import lax
from jax.sharding import PartitionSpec as P

D = 512
HD = 32
SIDE = 14
WIN = 7
SHIFT = 3
SEQ = 196
WSEQ = 49
TABLE = 169
LAYERS = 2


norm_eps = 1e-05
mask_fill = -100.0
beta_one = 0.9
beta_two = 0.999
adam_eps = 1e-08
learn_rate = 0.02
decay_rate = 0.05
adam_step = 3.0
root_half = 0.7071067811865476
inv_root_two_pi = 0.3989422804014327


def region_map():
    positions = jnp.arange(SIDE, dtype=jnp.int32)
    band = (positions >= SIDE - WIN).astype(jnp.int32) + (positions >= SIDE - SHIFT).astype(
        jnp.int32
    )
    return 3 * band[:, None] + band[None, :]


def to_windows(tensor, shifted):
    channels = tensor.shape[-1]
    num_images = tensor.shape[0] // SEQ
    across = SIDE // WIN
    layout = tensor.reshape(num_images, SIDE, SIDE, channels)
    if shifted:
        layout = jnp.roll(layout, (-SHIFT, -SHIFT), axis=(1, 2))
    layout = layout.reshape(num_images, across, WIN, across, WIN, channels).transpose(
        0, 1, 3, 2, 4, 5
    )
    return layout.reshape(num_images * across * across, WSEQ, channels)


def from_windows(tensor, shifted):
    channels = tensor.shape[-1]
    across = SIDE // WIN
    num_images = tensor.shape[0] // (across * across)
    layout = tensor.reshape(num_images, across, across, WIN, WIN, channels).transpose(
        0, 1, 3, 2, 4, 5
    )
    layout = layout.reshape(num_images, SIDE, SIDE, channels)
    if shifted:
        layout = jnp.roll(layout, (SHIFT, SHIFT), axis=(1, 2))
    return layout.reshape(num_images * SEQ, channels)


def split_heads(row_data, shifted, num_heads):
    windows = to_windows(row_data, shifted)
    return windows.reshape(windows.shape[0], WSEQ, num_heads, HD)


def merge_heads(windows, shifted):
    return from_windows(windows.reshape(windows.shape[0], WSEQ, -1), shifted)


def norm_forward(layer_in, gain_vec, shift_vec):
    row_mean = jnp.mean(layer_in, -1, keepdims=True)
    centered = layer_in - row_mean
    row_var = jnp.mean(centered * centered, -1, keepdims=True)
    inv_std = lax.rsqrt(row_var + norm_eps)
    norm_hat = centered * inv_std
    return (norm_hat * gain_vec + shift_vec, norm_hat, inv_std)


def norm_backward(grad_norm, norm_hat, inv_std, gain_vec):
    scaled = grad_norm * gain_vec
    grad_in = inv_std * (
        scaled
        - jnp.mean(scaled, -1, keepdims=True)
        - norm_hat * jnp.mean(scaled * norm_hat, -1, keepdims=True)
    )
    return (grad_in, jnp.sum(grad_norm * norm_hat, 0), jnp.sum(grad_norm, 0))


def gelu_value(pre_value):
    return pre_value * 0.5 * (1.0 + lax.erf(pre_value * root_half))


def gelu_slope(pre_value):
    return (
        0.5 * (1.0 + lax.erf(pre_value * root_half))
        + pre_value * jnp.exp(-0.5 * pre_value * pre_value) * inv_root_two_pi
    )


def head_bias(onehot_table, table_vals):
    picked = jnp.dot(onehot_table, table_vals, precision=lax.Precision.HIGHEST)
    return picked.T.reshape(table_vals.shape[1], WSEQ, WSEQ)


def attend(q_win, k_win, bias_heads, mask_add):
    scores = jnp.einsum(
        "wihd,wjhd->whij", q_win, k_win, preferred_element_type=jnp.float32
    ) * HD ** (-0.5)
    scores = scores + bias_heads[None]
    if mask_add is not None:
        shaped = (
            scores.reshape(-1, mask_add.shape[0], scores.shape[1], WSEQ, WSEQ)
            + mask_add[None, :, None]
        )
        scores = shaped.reshape(scores.shape)
    return jax.nn.softmax(scores, axis=-1)


def attention_forward(normed_b, weight_qkv, qv_vec, bias_heads, mask_add, shifted):
    num_heads = bias_heads.shape[0]
    head_cols = num_heads * HD
    qkv_rows = jnp.dot(
        normed_b, weight_qkv.reshape(D, 3 * head_cols), preferred_element_type=jnp.float32
    ).reshape(-1, 3, head_cols)
    query_b = (qkv_rows[:, 0] + qv_vec[0]).astype(jnp.bfloat16)
    key_b = qkv_rows[:, 1].astype(jnp.bfloat16)
    value_b = (qkv_rows[:, 2] + qv_vec[1]).astype(jnp.bfloat16)
    q_win = split_heads(query_b, shifted, num_heads)
    k_win = split_heads(key_b, shifted, num_heads)
    v_win = split_heads(value_b, shifted, num_heads)
    attn_probs = attend(q_win, k_win, bias_heads, mask_add)
    probs_b = attn_probs.astype(jnp.bfloat16)
    mixed_win = jnp.einsum(
        "whij,wjhd->wihd", probs_b, v_win, preferred_element_type=jnp.float32
    ).astype(jnp.bfloat16)
    return (q_win, k_win, v_win, merge_heads(mixed_win, shifted))


def layer_forward(layer_in, weights, qv_vec, one_vec, norm_rows, bias_heads, mask_add, shifted):
    weight_qkv, weight_proj, weight_one, weight_two = weights
    normed, hat_one, std_one = norm_forward(layer_in, norm_rows[0], norm_rows[1])
    normed_b = normed.astype(jnp.bfloat16)
    q_win, k_win, v_win, mixed_rows = attention_forward(
        normed_b, weight_qkv, qv_vec, bias_heads, mask_add, shifted
    )
    attn_part = jnp.dot(mixed_rows, weight_proj, preferred_element_type=jnp.float32)
    mid_state = (
        layer_in + lax.psum(attn_part.astype(jnp.bfloat16), "mp").astype(jnp.float32) + norm_rows[4]
    )
    hidden, hat_two, std_two = norm_forward(mid_state, norm_rows[2], norm_rows[3])
    hidden_b = hidden.astype(jnp.bfloat16)
    pre_value = jnp.dot(hidden_b, weight_one, preferred_element_type=jnp.float32) + one_vec
    act_b = gelu_value(pre_value).astype(jnp.bfloat16)
    mlp_part = jnp.dot(act_b, weight_two, preferred_element_type=jnp.float32)
    layer_out = (
        mid_state + lax.psum(mlp_part.astype(jnp.bfloat16), "mp").astype(jnp.float32) + norm_rows[5]
    )
    saved_list = (
        hat_one,
        std_one,
        normed_b,
        q_win,
        k_win,
        v_win,
        mixed_rows,
        hat_two,
        std_two,
        hidden_b,
        pre_value,
        act_b,
    )
    return (layer_out, saved_list)


def mlp_grads(grad_b, weight_one, weight_two, hidden_b, pre_value, act_b):
    grad_two = jnp.dot(act_b.T, grad_b, preferred_element_type=jnp.float32)
    grad_pre = jnp.dot(grad_b, weight_two.T, preferred_element_type=jnp.float32) * gelu_slope(
        pre_value
    )
    grad_pre_b = grad_pre.astype(jnp.bfloat16)
    grad_bias_one = jnp.sum(grad_pre, 0)
    grad_one = jnp.dot(hidden_b.T, grad_pre_b, preferred_element_type=jnp.float32)
    hidden_part = jnp.dot(grad_pre_b, weight_one.T, preferred_element_type=jnp.float32)
    return (grad_one, grad_two, grad_bias_one, hidden_part)


def attention_grads(
    mid_b,
    normed_b,
    q_win,
    k_win,
    v_win,
    mixed_rows,
    weight_qkv,
    weight_proj,
    bias_heads,
    mask_add,
    shifted,
    onehot_table,
):
    num_heads = bias_heads.shape[0]
    head_cols = num_heads * HD
    grad_proj = jnp.dot(mixed_rows.T, mid_b, preferred_element_type=jnp.float32)
    grad_mixed = jnp.dot(mid_b, weight_proj.T, preferred_element_type=jnp.float32).astype(
        jnp.bfloat16
    )
    gm_win = split_heads(grad_mixed, shifted, num_heads)
    attn_probs = attend(q_win, k_win, bias_heads, mask_add)
    probs_b = attn_probs.astype(jnp.bfloat16)
    grad_probs = jnp.einsum("wihd,wjhd->whij", gm_win, v_win, preferred_element_type=jnp.float32)
    grad_v = jnp.einsum("whij,wihd->wjhd", probs_b, gm_win, preferred_element_type=jnp.float32)
    grad_scores = attn_probs * (grad_probs - jnp.sum(grad_probs * attn_probs, -1, keepdims=True))
    pair_sums = jnp.sum(grad_scores, 0).reshape(num_heads, WSEQ * WSEQ)
    grad_table = jnp.dot(onehot_table.T, pair_sums.T, precision=lax.Precision.HIGHEST)
    scores_b = grad_scores.astype(jnp.bfloat16)
    grad_q = jnp.einsum(
        "whij,wjhd->wihd", scores_b, k_win, preferred_element_type=jnp.float32
    ) * HD ** (-0.5)
    grad_k = jnp.einsum(
        "whij,wihd->wjhd", scores_b, q_win, preferred_element_type=jnp.float32
    ) * HD ** (-0.5)
    q_rows = merge_heads(grad_q, shifted)
    k_rows = merge_heads(grad_k, shifted)
    v_rows = merge_heads(grad_v, shifted)
    grad_qv = jnp.stack([jnp.sum(q_rows, 0), jnp.sum(v_rows, 0)])
    grad_qkv_b = (
        jnp.stack([q_rows, k_rows, v_rows], axis=1).astype(jnp.bfloat16).reshape(-1, 3 * head_cols)
    )
    grad_qkv = jnp.dot(normed_b.T, grad_qkv_b, preferred_element_type=jnp.float32).reshape(
        D, 3, head_cols
    )
    normed_part = jnp.dot(
        grad_qkv_b, weight_qkv.reshape(D, 3 * head_cols).T, preferred_element_type=jnp.float32
    )
    return (grad_qkv, grad_proj, grad_qv, grad_table, normed_part)


def layer_backward(
    grad_out, saved_list, weights, norm_rows, bias_heads, mask_add, shifted, onehot_table
):
    (
        hat_one,
        std_one,
        normed_b,
        q_win,
        k_win,
        v_win,
        mixed_rows,
        hat_two,
        std_two,
        hidden_b,
        pre_value,
        act_b,
    ) = saved_list
    weight_qkv, weight_proj, weight_one, weight_two = weights
    grad_b = grad_out.astype(jnp.bfloat16)
    grad_bias_two = jnp.sum(grad_out, 0)
    grad_one, grad_two, grad_bias_one, hidden_part = mlp_grads(
        grad_b, weight_one, weight_two, hidden_b, pre_value, act_b
    )
    grad_hidden = lax.psum(hidden_part.astype(jnp.bfloat16), "mp").astype(jnp.float32)
    back_two, gain_two, shift_two = norm_backward(grad_hidden, hat_two, std_two, norm_rows[2])
    grad_mid = grad_out + back_two
    mid_b = grad_mid.astype(jnp.bfloat16)
    grad_bias_proj = jnp.sum(grad_mid, 0)
    grad_qkv, grad_proj, grad_qv, grad_table, normed_part = attention_grads(
        mid_b,
        normed_b,
        q_win,
        k_win,
        v_win,
        mixed_rows,
        weight_qkv,
        weight_proj,
        bias_heads,
        mask_add,
        shifted,
        onehot_table,
    )
    grad_normed = lax.psum(normed_part.astype(jnp.bfloat16), "mp").astype(jnp.float32)
    back_one, gain_one, shift_one = norm_backward(grad_normed, hat_one, std_one, norm_rows[0])
    grad_in = grad_mid + back_one
    norm_grads = jnp.stack(
        [gain_one, shift_one, gain_two, shift_two, grad_bias_proj, grad_bias_two]
    )
    return (
        grad_in,
        (grad_qkv, grad_proj, grad_one, grad_two),
        (grad_qv, grad_bias_one, grad_table, norm_grads),
    )


def adam_update(weight_in, moment_one, moment_two, grad_sum, decay):
    new_one = beta_one * moment_one + (1.0 - beta_one) * grad_sum
    new_two = beta_two * moment_two + (1.0 - beta_two) * grad_sum * grad_sum
    hat_one = new_one / (1.0 - beta_one**adam_step)
    hat_two = new_two / (1.0 - beta_two**adam_step)
    new_weight = weight_in - learn_rate * (
        hat_one / (jnp.sqrt(hat_two) + adam_eps) + decay * weight_in
    )
    return (new_weight, new_one, new_two)


def local(
    tokens,
    cotangent,
    image_count,
    rel_index,
    w_qkv,
    w_proj,
    w_fc_one,
    w_fc_two,
    qv_bias,
    fc_one_bias,
    rel_table,
    norm_vec,
    m_qkv,
    m_proj,
    m_fc_one,
    m_fc_two,
    m_qv_bias,
    m_fc_one_bias,
    m_rel_table,
    m_norm_vec,
    v_qkv,
    v_proj,
    v_fc_one,
    v_fc_two,
    v_qv_bias,
    v_fc_one_bias,
    v_rel_table,
    v_norm_vec,
):
    images_here = tokens.shape[0]
    total_rows = images_here * SEQ
    onehot_table = (
        rel_index.reshape(WSEQ * WSEQ)[:, None] == jnp.arange(TABLE, dtype=jnp.int32)[None, :]
    ).astype(jnp.float32)
    across = SIDE // WIN
    region_ids = region_map()
    region_win = (
        region_ids.reshape(across, WIN, across, WIN)
        .transpose(0, 2, 1, 3)
        .reshape(across * across, WSEQ)
    )
    mask_add = jnp.where(region_win[:, :, None] != region_win[:, None, :], mask_fill, 0.0).astype(
        jnp.float32
    )
    bias_list = [head_bias(onehot_table, rel_table[layer_idx]) for layer_idx in range(LAYERS)]
    live_mask = (jnp.arange(images_here, dtype=jnp.int32) < image_count[0]).astype(jnp.float32)
    layer_in = tokens.astype(jnp.float32).reshape(total_rows, D)
    saved_all = []
    kept = []
    for layer_idx in range(LAYERS):
        shifted = layer_idx % 2 == 1
        shards = (
            w_qkv[layer_idx].astype(jnp.bfloat16),
            w_proj[layer_idx].astype(jnp.bfloat16),
            w_fc_one[layer_idx].astype(jnp.bfloat16),
            w_fc_two[layer_idx].astype(jnp.bfloat16),
        )
        full_weights = (
            lax.all_gather(shards[0], "dp", axis=0, tiled=True),
            lax.all_gather(shards[1], "dp", axis=1, tiled=True),
            lax.all_gather(shards[2], "dp", axis=0, tiled=True),
            lax.all_gather(shards[3], "dp", axis=1, tiled=True),
        )
        kept.append(full_weights)
        layer_in, saved_list = layer_forward(
            layer_in,
            full_weights,
            qv_bias[layer_idx],
            fc_one_bias[layer_idx],
            norm_vec[layer_idx],
            bias_list[layer_idx],
            mask_add if shifted else None,
            shifted,
        )
        saved_all.append(saved_list)
    grad_out = (cotangent * live_mask[:, None, None]).reshape(total_rows, D)
    big_list = [None] * LAYERS
    small_list = [None] * LAYERS
    for layer_idx in reversed(range(LAYERS)):
        shifted = layer_idx % 2 == 1
        shards = (
            w_qkv[layer_idx].astype(jnp.bfloat16),
            w_proj[layer_idx].astype(jnp.bfloat16),
            w_fc_one[layer_idx].astype(jnp.bfloat16),
            w_fc_two[layer_idx].astype(jnp.bfloat16),
        )
        full_weights = (
            lax.all_gather(shards[0], "dp", axis=0, tiled=True),
            lax.all_gather(shards[1], "dp", axis=1, tiled=True),
            lax.all_gather(shards[2], "dp", axis=0, tiled=True),
            lax.all_gather(shards[3], "dp", axis=1, tiled=True),
        )
        grad_out, big_grads, small_list[layer_idx] = layer_backward(
            grad_out,
            saved_all[layer_idx],
            full_weights,
            norm_vec[layer_idx],
            bias_list[layer_idx],
            mask_add if shifted else None,
            shifted,
            onehot_table,
        )
        big_list[layer_idx] = (
            lax.psum_scatter(big_grads[0], "dp", scatter_dimension=0, tiled=True),
            lax.psum_scatter(big_grads[1], "dp", scatter_dimension=1, tiled=True),
            lax.psum_scatter(big_grads[2], "dp", scatter_dimension=0, tiled=True),
            lax.psum_scatter(big_grads[3], "dp", scatter_dimension=1, tiled=True),
        )
    stacked_small = tuple(
        (
            jnp.stack([small_list[layer_idx][slot] for layer_idx in range(LAYERS)])
            for slot in range(4)
        )
    )
    out_rows, grad_rows_all, norm_terms = (layer_in, grad_out, stacked_small[3])
    out = out_rows.reshape(images_here, SEQ, D)
    x_grad = grad_rows_all.reshape(images_here, SEQ, D)
    qv_grad, one_bias_grad, table_grad, norm_grad = lax.psum(
        (stacked_small[0], stacked_small[1], stacked_small[2], norm_terms), "dp"
    )
    qkv_grad = jnp.stack([big_list[layer_idx][0] for layer_idx in range(LAYERS)])
    proj_grad = jnp.stack([big_list[layer_idx][1] for layer_idx in range(LAYERS)])
    one_grad = jnp.stack([big_list[layer_idx][2] for layer_idx in range(LAYERS)])
    two_grad = jnp.stack([big_list[layer_idx][3] for layer_idx in range(LAYERS)])
    new_w_qkv, new_m_qkv, new_v_qkv = adam_update(w_qkv, m_qkv, v_qkv, qkv_grad, decay_rate)
    new_w_proj, new_m_proj, new_v_proj = adam_update(w_proj, m_proj, v_proj, proj_grad, decay_rate)
    new_w_fc_one, new_m_fc_one, new_v_fc_one = adam_update(
        w_fc_one, m_fc_one, v_fc_one, one_grad, decay_rate
    )
    new_w_fc_two, new_m_fc_two, new_v_fc_two = adam_update(
        w_fc_two, m_fc_two, v_fc_two, two_grad, decay_rate
    )
    new_qv_bias, new_m_qv_bias, new_v_qv_bias = adam_update(
        qv_bias, m_qv_bias, v_qv_bias, qv_grad, 0.0
    )
    new_fc_one_bias, new_m_fc_one_bias, new_v_fc_one_bias = adam_update(
        fc_one_bias, m_fc_one_bias, v_fc_one_bias, one_bias_grad, 0.0
    )
    new_rel_table, new_m_rel_table, new_v_rel_table = adam_update(
        rel_table, m_rel_table, v_rel_table, table_grad, 0.0
    )
    new_norm_vec, new_m_norm_vec, new_v_norm_vec = adam_update(
        norm_vec, m_norm_vec, v_norm_vec, norm_grad, 0.0
    )
    return (
        out,
        x_grad,
        new_w_qkv,
        new_w_proj,
        new_w_fc_one,
        new_w_fc_two,
        new_qv_bias,
        new_fc_one_bias,
        new_rel_table,
        new_norm_vec,
        new_m_qkv,
        new_m_proj,
        new_m_fc_one,
        new_m_fc_two,
        new_m_qv_bias,
        new_m_fc_one_bias,
        new_m_rel_table,
        new_m_norm_vec,
        new_v_qkv,
        new_v_proj,
        new_v_fc_one,
        new_v_fc_two,
        new_v_qv_bias,
        new_v_fc_one_bias,
        new_v_rel_table,
        new_v_norm_vec,
    )


def solution(mesh):
    return jax.shard_map(
        local,
        mesh=mesh,
        in_specs=(
            P("dp", None, None),
            P("dp", None, None),
            P("dp"),
            P(),
            P(None, "dp", None, "mp"),
            P(None, "mp", "dp"),
            P(None, "dp", "mp"),
            P(None, "mp", "dp"),
            P(None, None, "mp"),
            P(None, "mp"),
            P(None, None, "mp"),
            P(),
            P(None, "dp", None, "mp"),
            P(None, "mp", "dp"),
            P(None, "dp", "mp"),
            P(None, "mp", "dp"),
            P(None, None, "mp"),
            P(None, "mp"),
            P(None, None, "mp"),
            P(),
            P(None, "dp", None, "mp"),
            P(None, "mp", "dp"),
            P(None, "dp", "mp"),
            P(None, "mp", "dp"),
            P(None, None, "mp"),
            P(None, "mp"),
            P(None, None, "mp"),
            P(),
        ),
        out_specs=(
            P("dp", None, None),
            P("dp", None, None),
            P(None, "dp", None, "mp"),
            P(None, "mp", "dp"),
            P(None, "dp", "mp"),
            P(None, "mp", "dp"),
            P(None, None, "mp"),
            P(None, "mp"),
            P(None, None, "mp"),
            P(),
            P(None, "dp", None, "mp"),
            P(None, "mp", "dp"),
            P(None, "dp", "mp"),
            P(None, "mp", "dp"),
            P(None, None, "mp"),
            P(None, "mp"),
            P(None, None, "mp"),
            P(),
            P(None, "dp", None, "mp"),
            P(None, "mp", "dp"),
            P(None, "dp", "mp"),
            P(None, "mp", "dp"),
            P(None, None, "mp"),
            P(None, "mp"),
            P(None, None, "mp"),
            P(),
        ),
        check_vma=False,
    )
```

profile of v0, /device:TPU:0, one launch (start us, length us, event | category | flops | bytes accessed | tf_op | source)
XLA Modules:
  0.0 1680.7 jit_solution(12468175291455331147)
XLA Ops:
  14.0 49.4 %all-gather = bf16[1,512,3,256]{3,1,2,0:T(8,128)(2,1)} all-gather(bf16[1,32,3,256]{3,1,2,0:T(8,128)(2,1)S(1)} %get-tuple-element.155), channel_id=2, replica_groups=mesh['dp'=16,'mp'=2] {'dp'}, dimensions={1}, use_global_device_ids=true | all-gather | bytes 835584 | tf_op jit(solution)/shard_map/all_gather | solution.py:365
  80.2 37.3 %all-gather.1 = bf16[1,256,512]{1,2,0:T(8,128)(2,1)S(1)} all-gather(bf16[1,256,32]{1,2,0:T(8,128)(2,1)S(1)} %get-tuple-element.157), channel_id=3, replica_groups=mesh['dp'=16,'mp'=2] {'dp'}, dimensions={2}, use_global_device_ids=true | all-gather | bytes 278528 | tf_op jit(solution)/shard_map/all_gather | solution.py:366
  146.2 8.3 copy.145
  161.5 8.3 copy.142
  176.8 8.2 copy.143
  185.0 9.8 fusion.190
  194.8 8.5 convert_bitcast_fusion.1
  203.3 9.8 copy.147
  235.1 15.3 all-reduce.10.cloned.1.call-done
  257.5 30.0 %all-gather.13.cloned.1.call-done = bf16[1,512,1024]{2,1,0:T(8,128)(2,1)} async-done(((bf16[1,32,1024]{2,1,0:T(8,128)(2,1)}), bf16[1,512,1024]{2,1,0:T(8,128)(2,1)}) %all-gather.13.cloned.1.call-update) | async-done | bytes 1048592 | tf_op jit(solution)/shard_map/all_gather | solution.py:367
  287.5 9.3 multiply_convert_fusion.1
  296.8 47.9 %all-gather.15.cloned.1.call-done = bf16[1,1024,512]{1,2,0:T(8,128)(2,1)} async-done(((bf16[1,1024,32]{1,2,0:T(8,128)(2,1)}), bf16[1,1024,512]{1,2,0:T(8,128)(2,1)}) %all-gather.15.cloned.1.call-update) | async-done | bytes 1048592 | tf_op jit(solution)/shard_map/all_gather | solution.py:368
  354.0 43.1 %all-gather.4 = bf16[1,512,3,256]{3,1,2,0:T(8,128)(2,1)S(1)} all-gather(bf16[1,32,3,256]{3,1,2,0:T(8,128)(2,1)S(1)} %get-tuple-element.154), channel_id=6, replica_groups=mesh['dp'=16,'mp'=2] {'dp'}, dimensions={1}, use_global_device_ids=true | all-gather | bytes 835584 | tf_op jit(solution)/shard_map/all_gather | solution.py:365
  397.4 39.3 %all-gather.5 = bf16[1,256,512]{1,2,0:T(8,128)(2,1)} all-gather(bf16[1,256,32]{1,2,0:T(8,128)(2,1)S(1)} %get-tuple-element.156), channel_id=7, replica_groups=mesh['dp'=16,'mp'=2] {'dp'}, dimensions={2}, use_global_device_ids=true | all-gather | bytes 278528 | tf_op jit(solution)/shard_map/all_gather | solution.py:366
  476.2 8.3 copy.156
  502.8 8.6 copy.153
  512.7 9.9 fusion.191
  529.3 9.0 copy.158
  576.6 29.9 %all-gather.17.cloned.1.call-done = bf16[1,512,1024]{2,1,0:T(8,128)(2,1)} async-done(((bf16[1,32,1024]{2,1,0:T(8,128)(2,1)}), bf16[1,512,1024]{2,1,0:T(8,128)(2,1)}) %all-gather.17.cloned.1.call-update) | async-done | bytes 1048592 | tf_op jit(solution)/shard_map/all_gather | solution.py:367
  606.6 9.4 multiply_convert_fusion
  616.0 48.0 %all-gather.19.cloned.1.call-done = bf16[1,1024,512]{1,2,0:T(8,128)(2,1)} async-done(((bf16[1,1024,32]{1,2,0:T(8,128)(2,1)}), bf16[1,1024,512]{1,2,0:T(8,128)(2,1)}) %all-gather.19.cloned.1.call-update) | async-done | bytes 1048592 | tf_op jit(solution)/shard_map/all_gather | solution.py:368
  664.0 10.1 fusion.194
  680.6 20.8 %all-reduce.16.cloned.1.call-done = bf16[2352,512]{1,0:T(8,128)(2,1)} async-done(((bf16[2352,512]{1,0:T(8,128)(2,1)}), bf16[2352,512]{1,0:T(8,128)(2,1)}) %all-reduce.16.cloned.1.call-update) | async-done | bytes 2408464 | tf_op jit(solution)/shard_map/psum | solution.py:263
  729.5 10.8 fusion.73
  740.3 11.1 copy.173
  769.0 13.0 multiply_reduce_fusion.1
  782.0 9.5 fusion.53
  799.4 9.9 copy.169
  823.2 11.1 copy.165
  834.3 8.5 reshape_reshape.69
  877.3 22.9 %all-reduce.18.cloned.1.call-done = bf16[2352,512]{1,0:T(8,128)(2,1)} async-done(((bf16[2352,512]{1,0:T(8,128)(2,1)}), bf16[2352,512]{1,0:T(8,128)(2,1)}) %all-reduce.18.cloned.1.call-update) | async-done | bytes 2408464 | tf_op jit(solution)/shard_map/psum | solution.py:282
  931.2 18.7 %all-reduce.20.cloned.1.call-done = bf16[2352,512]{1,0:T(8,128)(2,1)} async-done(((bf16[2352,512]{1,0:T(8,128)(2,1)}), bf16[2352,512]{1,0:T(8,128)(2,1)}) %all-reduce.20.cloned.1.call-update) | async-done | bytes 2408464 | tf_op jit(solution)/shard_map/psum | solution.py:263
  966.8 8.3 fusion.109
  975.2 8.1 fusion.103
  983.4 8.2 fusion.82
  991.7 8.3 fusion.79
  1022.8 9.5 fusion.192
  1032.3 8.4 multiply_reduce_fusion
  1040.7 9.9 copy.188
  1059.5 9.5 fusion.55
  1074.8 9.1 copy.184
  1104.0 9.9 copy.180
  1166.0 80.0 %reduce-scatter.21.cloned.1.call-done = f32[1024,32]{0,1:T(8,128)} async-done(((f32[1024,512]{0,1:T(8,128)}), f32[1024,32]{0,1:T(8,128)}) %reduce-scatter.21.cloned.1.call-update) | async-done | bytes 131088 | tf_op jit(solution)/shard_map/reduce_scatter | solution.py:413
  1248.2 78.0 %reduce-scatter.19.cloned.1.call-done = f32[32,1024]{1,0:T(8,128)} async-done(((f32[512,1024]{1,0:T(8,128)}), f32[32,1024]{1,0:T(8,128)}) %reduce-scatter.19.cloned.1.call-update) | async-done | bytes 131088 | tf_op jit(solution)/shard_map/reduce_scatter | solution.py:412
  1326.3 80.4 %reduce-scatter.17.cloned.1.call-done = f32[32,1024]{1,0:T(8,128)} async-done(((f32[512,1024]{1,0:T(8,128)}), f32[32,1024]{1,0:T(8,128)}) %reduce-scatter.17.cloned.1.call-update) | async-done | bytes 131088 | tf_op jit(solution)/shard_map/reduce_scatter | solution.py:412
  1408.9 76.7 %reduce-scatter.11.cloned.1.call-done = f32[32,3,256]{2,0,1:T(8,128)} async-done(((f32[512,3,256]{2,0,1:T(8,128)}), f32[32,3,256]{2,0,1:T(8,128)}) %reduce-scatter.11.cloned.1.call-update) | async-done | bytes 98320 | tf_op jit(solution)/shard_map/reduce_scatter | solution.py:410
  1485.5 79.0 %reduce-scatter.9.cloned.1.call-done = f32[32,3,256]{2,0,1:T(8,128)} async-done(((f32[512,3,256]{2,0,1:T(8,128)}), f32[32,3,256]{2,0,1:T(8,128)}) %reduce-scatter.9.cloned.1.call-update) | async-done | bytes 98320 | tf_op jit(solution)/shard_map/reduce_scatter | solution.py:410
  1596.8 72.4 %all-reduce = (f32[2,2,256]{2,1,0:T(2,128)S(1)}, f32[2,1024]{1,0:T(2,128)S(1)}, f32[2,169,8]{1,2,0:T(8,128)S(1)}, f32[2,6,512]{2,1,0:T(8,128)S(1)}) all-reduce(f32[2,2,256]{2,1,0:T(2,128)S(1)} %pad_maximum_fusion.21, f32[2,1024]{1,0:T(2,128)S(1)} %pad_maximum_fusion.20, ...), channel_id=1, replica_groups=mesh['dp'=16,'mp'=2] {'dp'}, use_global_device_ids=true, to_apply=%region_44.45 | all-reduce | flops 11920 | bytes 95360 | tf_op jit(solution)/shard_map/psum | solution.py:424
  (531 shorter events, 512.5 us)
Async XLA Ops:
  8.1 242.3 %all-reduce.10.cloned.1.call-start = ((), (), s32[]{:S(2)}) async-start(), calls=%async_computation.8 | async-start | bytes 4816896 | tf_op jit(solution)/shard_map/psum | solution.py:150
  13.3 57.7 %copy-start.75 = (f32[12,196]{1,0:T(8,128)}, f32[12,196]{1,0:T(8,128)S(1)}, u32[]{:S(2)}) copy-start(f32[12,196]{1,0:T(8,128)S(1)} %add_rsqrt_fusion) | copy-start | bytes 28228
  13.9 57.1 %copy-start.89 = (f32[1,1,512]{2,0,1:T(1,128)}, f32[1,1,512]{2,0,1:T(1,128)S(1)}, u32[]{:S(2)}) copy-start(f32[1,1,512]{2,0,1:T(1,128)S(1)} %get-tuple-element.169) | copy-start | bytes 6148
  13.9 273.6 %copy-start.96 = (f32[1,1,512]{2,0,1:T(1,128)}, f32[1,1,512]{2,0,1:T(1,128)S(1)}, u32[]{:S(2)}) copy-start(f32[1,1,512]{2,0,1:T(1,128)S(1)} %get-tuple-element.166) | copy-start | bytes 6148
  13.9 273.6 %copy-start.121 = (f32[1,1,512]{2,0,1:T(1,128)}, f32[1,1,512]{2,0,1:T(1,128)S(1)}, u32[]{:S(2)}) copy-start(f32[1,1,512]{2,0,1:T(1,128)S(1)} %get-tuple-element.165) | copy-start | bytes 6148
  13.9 428.5 %copy-start.94 = (f32[1,1,512]{2,0,1:T(1,128)}, f32[1,1,512]{2,0,1:T(1,128)S(1)}, u32[]{:S(2)}) copy-start(f32[1,1,512]{2,0,1:T(1,128)S(1)} %get-tuple-element.163) | copy-start | bytes 6148
  13.9 428.5 %copy-start.119 = (f32[1,1,512]{2,0,1:T(1,128)}, f32[1,1,512]{2,0,1:T(1,128)S(1)}, u32[]{:S(2)}) copy-start(f32[1,1,512]{2,0,1:T(1,128)S(1)} %get-tuple-element.162) | copy-start | bytes 6148
  78.6 273.2 %copy-start.106 = (s32[2401]{0:T(1024)}, s32[2401]{0:T(1024)S(1)}, u32[]{:S(2)}) copy-start(s32[2401]{0:T(1024)S(1)} %eq.15) | copy-start | bytes 28816
  117.5 109.6 %copy-start.45 = (bf16[1,256,512]{1,2,0:T(8,128)(2,1)}, bf16[1,256,512]{1,2,0:T(8,128)(2,1)S(1)}, u32[]{:S(2)}) copy-start(bf16[1,256,512]{1,2,0:T(8,128)(2,1)S(1)} %all-gather.1) | copy-start | bytes 786436
  230.7 56.7 %all-gather.13.cloned.1.call-start = ((), (), s32[]{:S(2)}) async-start(), calls=%async_computation.22 | async-start | bytes 1114112 | tf_op jit(solution)/shard_map/all_gather | solution.py:367
  231.5 113.2 %all-gather.15.cloned.1.call-start = ((), (), s32[]{:S(2)}) async-start(), calls=%async_computation.23 | async-start | bytes 1114112 | tf_op jit(solution)/shard_map/all_gather | solution.py:368
  232.2 205.2 %all-reduce.12.cloned.1.call-start = ((), (), s32[]{:S(2)}) async-start(), calls=%async_computation.9 | async-start | bytes 4816896 | tf_op jit(solution)/shard_map/psum | solution.py:158
  351.5 218.0 %all-reduce.14.cloned.1.call-start = ((), (), s32[]{:S(2)}) async-start(), calls=%async_computation.10 | async-start | bytes 4816896 | tf_op jit(solution)/shard_map/psum | solution.py:150
  549.9 56.7 %all-gather.17.cloned.1.call-start = ((), (), s32[]{:S(2)}) async-start(), calls=%async_computation.24 | async-start | bytes 1114112 | tf_op jit(solution)/shard_map/all_gather | solution.py:367
  550.4 113.5 %all-gather.19.cloned.1.call-start = ((), (), s32[]{:S(2)}) async-start(), calls=%async_computation.25 | async-start | bytes 1114112 | tf_op jit(solution)/shard_map/all_gather | solution.py:368
  551.2 150.2 %all-reduce.16.cloned.1.call-start = ((), (), s32[]{:S(2)}) async-start(), calls=%async_computation.11 | async-start | bytes 4816896 | tf_op jit(solution)/shard_map/psum | solution.py:263
  573.4 134.2 %copy-start.73 = (f32[2352]{0:T(1024)}, f32[2352]{0:T(1024)S(1)}, u32[]{:S(2)}) copy-start(f32[2352]{0:T(1024)S(1)} %broadcast_multiply_fusion.10) | copy-start | bytes 28228
  576.6 131.1 %copy-start.81 = (f32[2352]{0:T(1024)}, f32[2352]{0:T(1024)S(1)}, u32[]{:S(2)}) copy-start(f32[2352]{0:T(1024)S(1)} %add_rsqrt_fusion.1) | copy-start | bytes 28228
  680.5 219.7 %all-reduce.18.cloned.1.call-start = ((), (), s32[]{:S(2)}) async-start(), calls=%async_computation.12 | async-start | bytes 4816896 | tf_op jit(solution)/shard_map/psum | solution.py:282
  766.3 89.8 %copy-start.28 = (f32[12,3,14,256]{3,2,1,0:T(8,128)}, f32[12,3,14,256]{3,2,1,0:T(8,128)S(1)}, u32[]{:S(2)}) copy-start(f32[12,3,14,256]{3,2,1,0:T(8,128)S(1)} %slice.372) | copy-start | bytes 1548292
  769.0 87.1 %copy-start.8 = (f32[12,11,14,256]{3,2,1,0:T(8,128)}, f32[12,11,14,256]{3,2,1,0:T(8,128)S(1)}, u32[]{:S(2)}) copy-start(f32[12,11,14,256]{3,2,1,0:T(8,128)S(1)} %slice.373) | copy-start | bytes 5677060
  877.1 72.8 %all-reduce.20.cloned.1.call-start = ((), (), s32[]{:S(2)}) async-start(), calls=%async_computation.13 | async-start | bytes 4816896 | tf_op jit(solution)/shard_map/psum | solution.py:263
  926.7 233.4 %reduce-scatter.15.cloned.1.call-start = ((), (), s32[]{:S(2)}) async-start(), calls=%async_computation.17 | async-start | bytes 557056 | tf_op jit(solution)/shard_map/reduce_scatter | solution.py:411
  931.1 229.0 %reduce-scatter.13.cloned.1.call-start = ((), (), s32[]{:S(2)}) async-start(), calls=%async_computation.16 | async-start | bytes 557056 | tf_op jit(solution)/shard_map/reduce_scatter | solution.py:411
  966.3 199.7 %reduce-scatter.23.cloned.1.call-start = ((), (), s32[]{:S(2)}) async-start(), calls=%async_computation.21 | async-start | bytes 2228224 | tf_op jit(solution)/shard_map/reduce_scatter | solution.py:413
  975.2 270.8 %reduce-scatter.21.cloned.1.call-start = ((), (), s32[]{:S(2)}) async-start(), calls=%async_computation.20 | async-start | bytes 2228224 | tf_op jit(solution)/shard_map/reduce_scatter | solution.py:413
  983.3 342.9 %reduce-scatter.19.cloned.1.call-start = ((), (), s32[]{:S(2)}) async-start(), calls=%async_computation.19 | async-start | bytes 2228224 | tf_op jit(solution)/shard_map/reduce_scatter | solution.py:412
  991.7 415.0 %reduce-scatter.17.cloned.1.call-start = ((), (), s32[]{:S(2)}) async-start(), calls=%async_computation.18 | async-start | bytes 2228224 | tf_op jit(solution)/shard_map/reduce_scatter | solution.py:412
  1000.1 485.4 %reduce-scatter.11.cloned.1.call-start = ((), (), s32[]{:S(2)}) async-start(), calls=%async_computation.15 | async-start | bytes 1671168 | tf_op jit(solution)/shard_map/reduce_scatter | solution.py:410
  1006.8 557.7 %reduce-scatter.9.cloned.1.call-start = ((), (), s32[]{:S(2)}) async-start(), calls=%async_computation.14 | async-start | bytes 1671168 | tf_op jit(solution)/shard_map/reduce_scatter | solution.py:410
  1133.5 432.8 %all-reduce.22.cloned.1.call-start = ((), (), s32[]{:S(2)}) async-start(), calls=%async_computation.26 | async-start | bytes 9633792 | tf_op jit(solution)/shard_map/psum | solution.py:158
  1149.6 414.9 %copy-start.58 = (f32[2,32,3,256]{3,1,2,0:T(8,128)S(1)}, f32[2,32,3,256]{3,1,2,0:T(8,128)}, u32[]{:S(2)}) copy-start(f32[2,32,3,256]{3,1,2,0:T(8,128)} %param.32) | copy-start | bytes 589828
  1151.7 412.8 %copy-start.67 = (f32[2,32,3,256]{3,1,2,0:T(8,128)S(1)}, f32[2,32,3,256]{3,1,2,0:T(8,128)}, u32[]{:S(2)}) copy-start(f32[2,32,3,256]{3,1,2,0:T(8,128)} %param.40) | copy-start | bytes 589828
  1151.8 412.8 %copy-start.68 = (f32[2,32,3,256]{3,1,2,0:T(8,128)S(1)}, f32[2,32,3,256]{3,1,2,0:T(8,128)}, u32[]{:S(2)}) copy-start(f32[2,32,3,256]{3,1,2,0:T(8,128)} %param.48) | copy-start | bytes 589828
  1151.8 414.6 %copy-start.83 = (f32[2352]{0:T(1024)S(1)}, f32[2352]{0:T(1024)}, u32[]{:S(2)}) copy-start(f32[2352]{0:T(1024)} %rsqrt.40) | copy-start | bytes 28228
  1151.8 414.6 %copy-start.90 = (f32[1,1,512]{2,0,1:T(1,128)S(1)}, f32[1,1,512]{2,0,1:T(1,128)}, u32[]{:S(2)}) copy-start(f32[1,1,512]{2,0,1:T(1,128)} %copy-done.89) | copy-start | bytes 6148
  1590.9 78.3 %copy-start.85 = (f32[2,6,512]{2,0,1:T(2,128)S(1)}, f32[2,6,512]{2,0,1:T(2,128)}, u32[]{:S(2)}) copy-start(f32[2,6,512]{2,0,1:T(2,128)} %param.39) | copy-start | bytes 73732
  1590.9 78.3 %copy-start.92 = (f32[2,6,512]{2,0,1:T(2,128)S(1)}, f32[2,6,512]{2,0,1:T(2,128)}, u32[]{:S(2)}) copy-start(f32[2,6,512]{2,0,1:T(2,128)} %param.47) | copy-start | bytes 73732
  1590.9 78.3 %copy-start.93 = (f32[2,6,512]{2,0,1:T(2,128)S(1)}, f32[2,6,512]{2,0,1:T(2,128)}, u32[]{:S(2)}) copy-start(f32[2,6,512]{2,0,1:T(2,128)} %param.55) | copy-start | bytes 73732
  1590.9 80.2 %copy-start.105 = (f32[2,2,256]{2,1,0:T(2,128)S(1)}, f32[2,2,256]{2,1,0:T(2,128)}, u32[]{:S(2)}) copy-start(f32[2,2,256]{2,1,0:T(2,128)} %param.36) | copy-start | bytes 12292
  1590.9 80.2 %copy-start.115 = (f32[2,2,256]{2,1,0:T(2,128)S(1)}, f32[2,2,256]{2,1,0:T(2,128)}, u32[]{:S(2)}) copy-start(f32[2,2,256]{2,1,0:T(2,128)} %param.44) | copy-start | bytes 12292
  1591.0 80.2 %copy-start.116 = (f32[2,2,256]{2,1,0:T(2,128)S(1)}, f32[2,2,256]{2,1,0:T(2,128)}, u32[]{:S(2)}) copy-start(f32[2,2,256]{2,1,0:T(2,128)} %param.52) | copy-start | bytes 12292
  1591.0 80.8 %copy-start.88 = (f32[2,1024]{1,0:T(2,128)S(1)}, f32[2,1024]{1,0:T(2,128)}, u32[]{:S(2)}) copy-start(f32[2,1024]{1,0:T(2,128)} %param.37) | copy-start | bytes 24580
  1591.0 80.8 %copy-start.110 = (f32[2,1024]{1,0:T(2,128)S(1)}, f32[2,1024]{1,0:T(2,128)}, u32[]{:S(2)}) copy-start(f32[2,1024]{1,0:T(2,128)} %param.45) | copy-start | bytes 24580
  1591.0 80.8 %copy-start.111 = (f32[2,1024]{1,0:T(2,128)S(1)}, f32[2,1024]{1,0:T(2,128)}, u32[]{:S(2)}) copy-start(f32[2,1024]{1,0:T(2,128)} %param.53) | copy-start | bytes 24580
  1591.0 81.4 %copy-start.101 = (f32[2,169,8]{1,2,0:T(8,128)S(1)}, f32[2,169,8]{1,2,0:T(8,128)}, u32[]{:S(2)}) copy-start(f32[2,169,8]{1,2,0:T(8,128)} %param.38) | copy-start | bytes 32452
  1591.0 81.4 %copy-start.102 = (f32[2,169,8]{1,2,0:T(8,128)S(1)}, f32[2,169,8]{1,2,0:T(8,128)}, u32[]{:S(2)}) copy-start(f32[2,169,8]{1,2,0:T(8,128)} %param.46) | copy-start | bytes 32452
  1591.0 81.4 %copy-start.103 = (f32[2,169,8]{1,2,0:T(8,128)S(1)}, f32[2,169,8]{1,2,0:T(8,128)}, u32[]{:S(2)}) copy-start(f32[2,169,8]{1,2,0:T(8,128)} %param.54) | copy-start | bytes 32452
  (106 other events, 1082.1 us)
Sparse Core Ops, SparseCore 0:
  230.8 19.5 all-reduce.9
  351.7 20.6 all-reduce.11
  550.0 19.4 all-reduce.13
  680.6 20.6 all-reduce.15
  877.2 23.0 all-reduce.17
  926.8 23.0 all-reduce.19
  1144.8 30.3 all-reduce.21
Sparse Core Ops, SparseCore 1:
  234.5 52.9 all-gather.12
  290.7 54.0 all-gather.14
  553.7 52.8 all-gather.16
  609.9 54.0 all-gather.18
  931.2 78.7 reduce-scatter.14
  1012.2 73.8 reduce-scatter.12
  1088.2 77.8 reduce-scatter.22
  1168.2 77.8 reduce-scatter.20
  1248.2 78.0 reduce-scatter.18
  1328.6 78.0 reduce-scatter.16
  1408.8 76.7 reduce-scatter.10
  1487.8 76.6 reduce-scatter.8
where the time goes:
time: 1690 us; the launch traced here: 1680 us
  waiting for transfers between devices  638 us (38%)
  local copies, waits for them, and re-layouts  408 us (24%)
  blocking collectives  242 us (14%)
  matrix products  234 us (14%)
  other arithmetic  139 us (8%)
  between operations  18.4 us (1%)
    reduce_scatter x2, waiting for transfers between devices, local(): lax.psum_scatter(big_grads[2], 'dp', scatter_dimension=0, tiled=True)  158 us
    reduce_scatter x2, waiting for transfers between devices, local(): lax.psum_scatter(big_grads[0], 'dp', scatter_dimension=0, tiled=True)  156 us
    another operation x16, local copies, waits for them, and re-layouts, split_heads(): return windows.reshape(windows.shape[0], WSEQ, num_heads, HD)  107 us
    all_gather x2, waiting for transfers between devices, local(): lax.all_gather(shards[3], 'dp', axis=1, tiled=True)  95.9 us
    all_gather x2, blocking collectives, local(): lax.all_gather(shards[0], 'dp', axis=0, tiled=True)  92.5 us
    reduce_scatter x2, waiting for transfers between devices, local(): lax.psum_scatter(big_grads[3], 'dp', scatter_dimension=1, tiled=True)  84.2 us
    all_gather x2, blocking collectives, local(): lax.all_gather(shards[1], 'dp', axis=1, tiled=True)  76.6 us
    psum x1, blocking collectives, local(): lax.psum((stacked_small[0], stacked_small[1], stacked_small[2], norm_term...  72.4 us
  transfers between devices with their start and end apart: 19, of which 15 were waited for; matrix products, arithmetic and copies ran while one was open for 16% of the time, Pallas kernels for 0%

commit v1 on v0

v1 whole, which is shorter than its diff:
```python
import functools

import jax
import jax.numpy as jnp
import numpy as np
from jax import lax
from jax.experimental import pallas as pl
from jax.experimental.pallas import tpu as pltpu
from jax.sharding import PartitionSpec as P

D = 512
HD = 32
SIDE = 14
WIN = 7
SHIFT = 3
SEQ = 196
WSEQ = 49
TABLE = 169
LAYERS = 2
SEQP = 200
PAIR = 2
ROWS = PAIR * SEQP
WROW = 64
WIMG = 4 * WROW
WPAIR = PAIR * WIMG
HALF = 256
GROUP = 8
LANES = GROUP * WROW
FFH = 1024
QKV = 3 * HALF
COLS = 2 * FFH + QKV + HALF
ATT = 2 * FFH

norm_eps = 1e-05
mask_fill = -100.0
pad_fill = -1e30
beta_one = 0.9
beta_two = 0.999
adam_eps = 1e-08
learn_rate = 0.02
decay_rate = 0.05
adam_step = 3.0
root_half = 0.7071067811865476
inv_root_two_pi = 0.3989422804014327
score_scale = HD**-0.5

f32 = jnp.float32
bf16 = jnp.bfloat16


def dot(a, b, ca=1, cb=0):
    return lax.dot_general(a, b, (((ca,), (cb,)), ((), ())), preferred_element_type=f32)


def window_tokens(shifted):
    off = SHIFT if shifted else 0
    out = np.zeros((4, WSEQ), np.int64)
    for wr in range(2):
        for wc in range(2):
            for p in range(WSEQ):
                r = (7 * wr + p // 7 + off) % SIDE
                c = (7 * wc + p % 7 + off) % SIDE
                out[wr * 2 + wc, p] = r * SIDE + c
    return out


def permutation(shifted):
    tok = window_tokens(shifted)
    perm = np.zeros((WIMG, SEQP), np.float32)
    for w in range(4):
        perm[w * WROW + np.arange(WSEQ), tok[w]] = 1.0
    return perm


def region_mask():
    pos = np.arange(SIDE)
    band = (pos >= SIDE - WIN).astype(int) + (pos >= SIDE - SHIFT).astype(int)
    region = 3 * band[:, None] + band[None, :]
    win = region.reshape(2, WIN, 2, WIN).transpose(0, 2, 1, 3).reshape(4, WSEQ)
    out = np.zeros((4, WROW, WROW), np.float32)
    out[:, :WSEQ, :WSEQ] = np.where(win[:, :, None] != win[:, None, :], mask_fill, 0.0)
    return out


def norm_stats(z):
    mean = jnp.mean(z, -1, keepdims=True)
    cen = z - mean
    var = jnp.mean(cen * cen, -1, keepdims=True)
    inv = lax.rsqrt(var + norm_eps)
    return cen * inv, inv


def norm_back(e, hat, inv, gain):
    s = e * gain
    return inv * (s - jnp.mean(s, -1, keepdims=True) - hat * jnp.mean(s * hat, -1, keepdims=True))


def row_sum(v):
    return jnp.sum(v, 0, keepdims=True)


def put_images(ref, blk):
    for im in range(PAIR):
        ref[im * SEQP : im * SEQP + SEQ, :] = blk[im].astype(f32)
        ref[im * SEQP + SEQ : (im + 1) * SEQP, :] = jnp.zeros((SEQP - SEQ, D), f32)


def to_window_rows(perm, rows, out_ref):
    for im in range(PAIR):
        part = rows[im * SEQP : (im + 1) * SEQP].astype(bf16)
        out_ref[im * WIMG : (im + 1) * WIMG, :] = dot(perm, part).astype(bf16)


def to_token_rows(perm_t, ref):
    return jnp.concatenate(
        [dot(perm_t, ref[im * WIMG : (im + 1) * WIMG, :]) for im in range(PAIR)], 0
    ).astype(bf16)


def expand_heads(x, hm_ref):
    return jnp.concatenate([x * hm_ref[h : h + 1, :] for h in range(GROUP)], 0)


def fold_heads(o):
    lane = lax.broadcasted_iota(jnp.int32, (WROW, HALF), 1) // HD
    acc = o[:WROW]
    for h in range(1, GROUP):
        acc = jnp.where(lane == h, o[h * WROW : (h + 1) * WROW], acc)
    return acc


def softmax_cols(k, qx, bias):
    s = dot(k, qx, 1, 1) * score_scale + bias
    e = jnp.exp(s - jnp.max(s, 0, keepdims=True))
    return e * (1.0 / jnp.sum(e, 0, keepdims=True))


def attend_forward(x, w_ref, bias_ref, qvb_ref, nv_ref, perm_ref, perm_t_ref, hm_ref,
                   qkv_ref, mixed_ref, nperm, mixw, windows):
    hat, _ = norm_stats(x)
    normed = hat * nv_ref[0:1, :] + nv_ref[1:2, :]
    to_window_rows(perm_ref[...], normed, nperm)
    for m in range(2):
        r = dot(nperm[...], w_ref[m, :, :QKV])
        qkv_ref[:, m * QKV : (m + 1) * QKV] = (r + qvb_ref[m : m + 1, :]).astype(bf16)

    def body(w, carry):
        rows = pl.ds(pl.multiple_of(w * WROW, WROW), WROW)
        wt = lax.rem(w, windows) if windows > 1 else 0
        for m in range(2):
            base = m * QKV
            q = qkv_ref[rows, base : base + HALF]
            k = qkv_ref[rows, base + HALF : base + 2 * HALF]
            v = qkv_ref[rows, base + 2 * HALF : base + QKV]
            pr = softmax_cols(k, expand_heads(q, hm_ref), bias_ref[wt, m])
            o = dot(pr.astype(bf16), v, 0, 0)
            mixw[rows, m * HALF : (m + 1) * HALF] = fold_heads(o).astype(bf16)
        return carry

    lax.fori_loop(0, 4 * PAIR, body, 0)
    mixed = to_token_rows(perm_t_ref[...], mixw)
    mixed_ref[...] = mixed
    attn = dot(mixed[:, :HALF], w_ref[0, :, QKV:], 1, 1) + dot(mixed[:, HALF:], w_ref[1, :, QKV:], 1, 1)
    return x + attn + nv_ref[4:5, :]


CH = 512


def mlp_forward(mid, w_ref, b1_ref, nv_ref, act_ref, slope_ref):
    hat, _ = norm_stats(mid)
    hid = (hat * nv_ref[2:3, :] + nv_ref[3:4, :]).astype(bf16)
    total = jnp.zeros((ROWS, D), f32)
    for m in range(2):
        for c in range(0, FFH, CH):
            col = m * FFH + c
            u = dot(hid, w_ref[m, :, c : c + CH]) + b1_ref[:, col : col + CH]
            phi = 0.5 + 0.5 * lax.erf(u * root_half)
            act = (u * phi).astype(bf16)
            act_ref[:, col : col + CH] = act
            slope_ref[:, col : col + CH] = (phi + u * jnp.exp(-0.5 * u * u) * inv_root_two_pi).astype(bf16)
            total += dot(act, w_ref[m, :, FFH + c : FFH + c + CH], 1, 1)
    return mid + total + nv_ref[5:6, :]


def mlp_backward(gout, mid, w_ref, nv_ref, slope_ref, gp, hid_s, gb_s, rows, b1_acc, nv_acc):
    hat, inv = norm_stats(mid)
    hid_s[rows, :] = (hat * nv_ref[2:3, :] + nv_ref[3:4, :]).astype(bf16)
    gb = gout.astype(bf16)
    gb_s[rows, :] = gb
    ghid = jnp.zeros((ROWS, D), f32)
    for m in range(2):
        for c in range(0, FFH, CH):
            col = m * FFH + c
            g = dot(gb, w_ref[m, :, FFH + c : FFH + c + CH]) * slope_ref[:, col : col + CH].astype(f32)
            b1_acc[:, col : col + CH] += row_sum(g)
            g = g.astype(bf16)
            gp[rows, col : col + CH] = g
            ghid += dot(g, w_ref[m, :, c : c + CH], 1, 1)
    gmid = gout + norm_back(ghid, hat, inv, nv_ref[2:3, :])
    nv_acc[2:3, :] += row_sum(ghid * hat)
    nv_acc[3:4, :] += row_sum(ghid)
    nv_acc[4:5, :] += row_sum(gmid)
    nv_acc[5:6, :] += row_sum(gout)
    return gmid


def attend_backward(gmid, x, w_ref, bias_ref, nv_ref, perm_ref, perm_t_ref, hm_ref, qkv_ref,
                    mperm, gmw, gqw, gq_s, mb_s, nb_s, rows, ds_acc, qv_acc, nv_acc, windows):
    hat, inv = norm_stats(x)
    nb_s[rows, :] = (hat * nv_ref[0:1, :] + nv_ref[1:2, :]).astype(bf16)
    mb_s[rows, :] = gmid.astype(bf16)
    to_window_rows(perm_ref[...], gmid, mperm)
    for m in range(2):
        gmw[:, m * HALF : (m + 1) * HALF] = dot(mperm[...], w_ref[m, :, QKV:]).astype(bf16)

    def body(w, carry):
        wrows = pl.ds(pl.multiple_of(w * WROW, WROW), WROW)
        wt = lax.rem(w, windows) if windows > 1 else 0
        for m in range(2):
            base = m * QKV
            q = qkv_ref[wrows, base : base + HALF]
            k = qkv_ref[wrows, base + HALF : base + 2 * HALF]
            v = qkv_ref[wrows, base + 2 * HALF : base + QKV]
            gm = gmw[wrows, m * HALF : (m + 1) * HALF]
            qx = expand_heads(q, hm_ref)
            gx = expand_heads(gm, hm_ref)
            pr = softmax_cols(k, qx, bias_ref[wt, m])
            dp = dot(v, gx, 1, 1)
            ds = pr * (dp - jnp.sum(pr * dp, 0, keepdims=True))
            ds_acc[m] += ds
            ds = ds.astype(bf16)
            gv = dot(pr.astype(bf16), gx)
            gk = dot(ds, qx) * score_scale
            gq = fold_heads(dot(ds, k, 0, 0)) * score_scale
            qv_acc[0:1, m * HALF : (m + 1) * HALF] += row_sum(gq)
            qv_acc[1:2, m * HALF : (m + 1) * HALF] += row_sum(gv)
            gqw[wrows, base : base + HALF] = gq.astype(bf16)
            gqw[wrows, base + HALF : base + 2 * HALF] = gk.astype(bf16)
            gqw[wrows, base + 2 * HALF : base + QKV] = gv.astype(bf16)
        return carry

    lax.fori_loop(0, 4 * PAIR, body, 0)
    gq = to_token_rows(perm_t_ref[...], gqw)
    gq_s[rows, :] = gq
    gnorm = dot(gq[:, :QKV], w_ref[0, :, :QKV], 1, 1) + dot(gq[:, QKV:], w_ref[1, :, :QKV], 1, 1)
    nv_acc[0:1, :] += row_sum(gnorm * hat)
    nv_acc[1:2, :] += row_sum(gnorm)
    return gmid + norm_back(gnorm, hat, inv, nv_ref[0:1, :])


def forward_kernel(first, last, windows, x_ref, wm_ref, wa_ref, bias_ref, qvb_ref, b1_ref, nv_ref,
                   perm_ref, perm_t_ref, hm_ref, y_ref, mid_ref, qkv_ref, mixed_ref, act_ref, slope_ref,
                   xs, nperm, mixw):
    if first:
        put_images(xs, x_ref)
        x = xs[...]
    else:
        x = x_ref[...]
    mid = attend_forward(x, wa_ref, bias_ref, qvb_ref, nv_ref, perm_ref, perm_t_ref, hm_ref,
                         qkv_ref, mixed_ref, nperm, mixw, windows)
    mid_ref[...] = mid
    y = mlp_forward(mid, wm_ref, b1_ref, nv_ref, act_ref, slope_ref)
    if last:
        for im in range(PAIR):
            y_ref[im] = y[im * SEQP : im * SEQP + SEQ]
    else:
        y_ref[...] = y


GW = 1024


def backward_kernel(first, last, windows, steps, g_ref, x_ref, mid_ref, wm_ref, wa_ref, bias_ref, nv_ref,
                    perm_ref, perm_t_ref, hm_ref, live_ref, qkv_ref, slope_ref, act_ref, mixed_ref,
                    gx_ref, gw_ref, qv_acc, b1_acc, ds_acc, nv_acc,
                    xs, gs, mperm, gmw, gqw, gp, gq_s, hid_s, gb_s, mb_s, nb_s):
    i = pl.program_id(0)

    @pl.when(i == 0)
    def _():
        for ref in (qv_acc, b1_acc, ds_acc, nv_acc):
            ref[...] = jnp.zeros_like(ref)

    @pl.when(i < steps)
    def _():
        rows = pl.ds(pl.multiple_of(i * ROWS, ROWS), ROWS)
        if last:
            for im in range(PAIR):
                flag = live_ref[im : im + 1, :]
                gs[im * SEQP : im * SEQP + SEQ, :] = g_ref[im] * jnp.concatenate([flag] * 4, 1)
                gs[im * SEQP + SEQ : (im + 1) * SEQP, :] = jnp.zeros((SEQP - SEQ, D), f32)
            gout = gs[...]
        else:
            gout = g_ref[...]
        if first:
            put_images(xs, x_ref)
            x = xs[...]
        else:
            x = x_ref[...]
        gmid = mlp_backward(gout, mid_ref[...], wm_ref, nv_ref, slope_ref, gp, hid_s, gb_s, rows, b1_acc, nv_acc)
        gin = attend_backward(gmid, x, wa_ref, bias_ref, nv_ref, perm_ref, perm_t_ref, hm_ref, qkv_ref,
                              mperm, gmw, gqw, gq_s, mb_s, nb_s, rows, ds_acc, qv_acc, nv_acc, windows)
        if first:
            for im in range(PAIR):
                gx_ref[im] = gin[im * SEQP : im * SEQP + SEQ]
        else:
            gx_ref[...] = gin

    for m in range(2):

        @pl.when(i == steps + 3 * m)
        def _():
            gw_ref[0] = dot(hid_s[...], gp[:, m * FFH : (m + 1) * FFH], 0, 0).astype(bf16)

        @pl.when(i == steps + 3 * m + 1)
        def _():
            gw_ref[0] = dot(gb_s[...], act_ref[:, m * FFH : (m + 1) * FFH], 0, 0).astype(bf16)

        @pl.when(i == steps + 3 * m + 2)
        def _():
            gw_ref[0, :, :QKV] = dot(nb_s[...], gq_s[:, m * QKV : (m + 1) * QKV], 0, 0).astype(bf16)
            gw_ref[0, :, QKV:] = dot(mb_s[...], mixed_ref[:, m * HALF : (m + 1) * HALF], 0, 0).astype(bf16)


def whole(shape, buffers=1):
    zero = (0,) * len(shape)
    return pl.BlockSpec(shape, lambda i: zero, pipeline_mode=pl.Buffered(buffers))


VLIM = 60 * 1024 * 1024


def forward_layer(layer, x, wg, bias, qvb, b1, nv, consts, steps):
    first, last = layer == 0, layer == LAYERS - 1
    shifted = layer % 2 == 1
    perm, perm_t, hm = consts
    nimg = steps * PAIR
    windows = bias.shape[0]
    img = lambda: pl.BlockSpec((PAIR, SEQ, D), lambda i: (i, 0, 0))
    row = lambda n: pl.BlockSpec((ROWS, n), lambda i: (i, 0))
    return pl.pallas_call(
        functools.partial(forward_kernel, first, last, windows),
        name=f"forward_{layer}",
        grid=(steps,),
        in_specs=[
            img() if first else row(D),
            pl.BlockSpec((2, D, ATT), lambda i: (0, 0, 0), pipeline_mode=pl.Buffered(1)),
            pl.BlockSpec((2, D, COLS - ATT), lambda i: (0, 0, ATT // (COLS - ATT)), pipeline_mode=pl.Buffered(1)),
            whole(bias.shape), whole(qvb.shape), whole(b1.shape), whole(nv.shape),
            whole(perm.shape), whole(perm_t.shape), whole(hm.shape),
        ],
        out_specs=[
            img() if last else row(D), row(D),
            pl.BlockSpec((WPAIR, 2 * QKV), lambda i: (i, 0)), row(D), row(2 * FFH), row(2 * FFH),
        ],
        out_shape=[
            jax.ShapeDtypeStruct((nimg, SEQ, D) if last else (nimg * SEQP, D), f32),
            jax.ShapeDtypeStruct((nimg * SEQP, D), f32),
            jax.ShapeDtypeStruct((steps * WPAIR, 2 * QKV), bf16),
            jax.ShapeDtypeStruct((nimg * SEQP, D), bf16),
            jax.ShapeDtypeStruct((nimg * SEQP, 2 * FFH), bf16),
            jax.ShapeDtypeStruct((nimg * SEQP, 2 * FFH), bf16),
        ],
        scratch_shapes=[
            pltpu.VMEM((ROWS, D), f32), pltpu.VMEM((WPAIR, D), bf16), pltpu.VMEM((WPAIR, D), bf16),
        ],
        compiler_params=pltpu.CompilerParams(vmem_limit_bytes=VLIM),
    )(x, wg, wg, bias, qvb, b1, nv, perm, perm_t, hm)


def backward_layer(layer, grad, x, saved, wg, bias, nv, consts, live, steps):
    first, last = layer == 0, layer == LAYERS - 1
    perm, perm_t, hm = consts
    mid, qkv, mixed, act, slope = saved
    nimg = steps * PAIR
    windows = bias.shape[0]
    top = steps - 1
    img = lambda: pl.BlockSpec((PAIR, SEQ, D), lambda i: (jnp.minimum(i, top), 0, 0))
    row = lambda n: pl.BlockSpec((ROWS, n), lambda i: (jnp.minimum(i, top), 0))
    total = nimg * SEQP

    def gmap(i):
        k = jnp.maximum(i - steps, 0)
        return (k // 3, 0, lax.rem(k, 3))

    return pl.pallas_call(
        functools.partial(backward_kernel, first, last, windows, steps),
        name=f"backward_{layer}",
        grid=(steps + 6,),
        in_specs=[
            img() if last else row(D), img() if first else row(D), row(D),
            pl.BlockSpec((2, D, ATT), lambda i: (0, 0, 0), pipeline_mode=pl.Buffered(1)),
            pl.BlockSpec((2, D, COLS - ATT), lambda i: (0, 0, ATT // (COLS - ATT)), pipeline_mode=pl.Buffered(1)),
            whole(bias.shape), whole(nv.shape), whole(perm.shape), whole(perm_t.shape), whole(hm.shape),
            pl.BlockSpec((None, PAIR, 128), lambda i: (jnp.minimum(i, top), 0, 0)),
            pl.BlockSpec((WPAIR, 2 * QKV), lambda i: (jnp.minimum(i, top), 0)), row(2 * FFH),
            whole(act.shape), whole(mixed.shape),
        ],
        out_specs=[
            img() if first else row(D),
            pl.BlockSpec((1, D, GW), gmap),
            whole((2, 2 * HALF)), whole((1, 2 * FFH)), whole((2, WROW, LANES)), whole((8, D)),
        ],
        out_shape=[
            jax.ShapeDtypeStruct((nimg, SEQ, D) if first else (total, D), f32),
            jax.ShapeDtypeStruct((2, D, COLS), bf16),
            jax.ShapeDtypeStruct((2, 2 * HALF), f32),
            jax.ShapeDtypeStruct((1, 2 * FFH), f32),
            jax.ShapeDtypeStruct((2, WROW, LANES), f32),
            jax.ShapeDtypeStruct((8, D), f32),
        ],
        scratch_shapes=[
            pltpu.VMEM((ROWS, D), f32), pltpu.VMEM((ROWS, D), f32),
            pltpu.VMEM((WPAIR, D), bf16), pltpu.VMEM((WPAIR, D), bf16), pltpu.VMEM((WPAIR, 2 * QKV), bf16),
            pltpu.VMEM((total, 2 * FFH), bf16), pltpu.VMEM((total, 2 * QKV), bf16),
            pltpu.VMEM((total, D), bf16), pltpu.VMEM((total, D), bf16),
            pltpu.VMEM((total, D), bf16), pltpu.VMEM((total, D), bf16),
        ],
        compiler_params=pltpu.CompilerParams(vmem_limit_bytes=VLIM),
    )(grad, x, mid, wg, wg, bias, nv, perm, perm_t, hm, live, qkv, slope, act, mixed)


def head_mask():
    return (np.arange(HALF)[None, :] // HD == np.arange(GROUP)[:, None]).astype(np.float32)


def bias_cols(onehot, table, shifted):
    picked = jnp.dot(table.T, onehot, precision=lax.Precision.HIGHEST).reshape(2, GROUP, WSEQ, WSEQ)
    by_j = picked.transpose(0, 3, 1, 2)
    by_j = jnp.pad(by_j, ((0, 0), (0, 0), (0, 0), (0, WROW - WSEQ)))
    by_j = jnp.pad(by_j, ((0, 0), (0, WROW - WSEQ), (0, 0), (0, 0)), constant_values=pad_fill)
    if shifted:
        by_j = by_j[None] + jnp.asarray(region_mask())[:, None, :, None, :]
    else:
        by_j = by_j[None]
    return by_j.reshape(-1, 2, WROW, LANES)


def adam_update(weight_in, moment_one, moment_two, grad_sum, decay):
    new_one = beta_one * moment_one + (1.0 - beta_one) * grad_sum
    new_two = beta_two * moment_two + (1.0 - beta_two) * grad_sum * grad_sum
    hat_one = new_one / (1.0 - beta_one**adam_step)
    hat_two = new_two / (1.0 - beta_two**adam_step)
    new_weight = weight_in - learn_rate * (hat_one / (jnp.sqrt(hat_two) + adam_eps) + decay * weight_in)
    return (new_weight, new_one, new_two)


def both_halves(mine, me):
    other = lax.ppermute(mine, "mp", [(0, 1), (1, 0)])
    low = jnp.where(me == 0, mine, other)
    high = jnp.where(me == 0, other, mine)
    return jnp.concatenate([low, high], 0)


def local(
    tokens, cotangent, image_count, rel_index,
    w_qkv, w_proj, w_fc_one, w_fc_two, qv_bias, fc_one_bias, rel_table, norm_vec,
    m_qkv, m_proj, m_fc_one, m_fc_two, m_qv_bias, m_fc_one_bias, m_rel_table, m_norm_vec,
    v_qkv, v_proj, v_fc_one, v_fc_two, v_qv_bias, v_fc_one_bias, v_rel_table, v_norm_vec,
):
    me = lax.axis_index("mp")
    images = tokens.shape[0]
    nimg = images // 2
    steps = nimg // PAIR
    part = w_qkv.shape[1]
    tok = lax.dynamic_slice_in_dim(tokens, me * nimg, nimg, 0)
    cot = lax.dynamic_slice_in_dim(cotangent, me * nimg, nimg, 0)
    live = (jnp.arange(nimg, dtype=jnp.int32) + me * nimg < image_count[0]).astype(f32)
    live = jnp.broadcast_to(live[:, None], (nimg, 128)).reshape(steps, PAIR, 128)

    packed = jnp.concatenate(
        [w_fc_one, w_fc_two.transpose(0, 2, 1), w_qkv.reshape(LAYERS, part, QKV), w_proj.transpose(0, 2, 1)], 2
    ).astype(bf16)
    gathered = lax.all_gather(packed, ("mp", "dp"))
    small = jnp.concatenate(
        [qv_bias.reshape(LAYERS, -1), fc_one_bias, rel_table.reshape(LAYERS, -1)], 1
    )
    small = lax.all_gather(small, "mp")
    qvb = small[:, :, : 2 * HALF].reshape(2, LAYERS, 2, HALF)
    b1 = small[:, :, 2 * HALF : 2 * HALF + FFH].transpose(1, 0, 2).reshape(LAYERS, 1, 2 * FFH)
    table = small[:, :, 2 * HALF + FFH :].reshape(2, LAYERS, TABLE, GROUP).transpose(1, 2, 0, 3)
    table = table.reshape(LAYERS, TABLE, 2 * GROUP)
    qvb = jnp.concatenate([qvb[:, :, 0], jnp.zeros_like(qvb[:, :, 0]), qvb[:, :, 1]], 2)

    onehot = (rel_index.reshape(1, WSEQ * WSEQ) == jnp.arange(TABLE, dtype=jnp.int32)[:, None]).astype(f32)
    hm = jnp.asarray(head_mask(), bf16)
    x, xs, saved, ctx = tok, [], [], []
    for layer in range(LAYERS):
        shifted = layer % 2 == 1

        wg = gathered.reshape(2, -1, LAYERS, part, COLS)[:, :, layer]
        wg = wg.reshape(2, D, COLS)
        bias = bias_cols(onehot, table[layer], shifted)
        p = permutation(shifted)
        consts = (jnp.asarray(p, bf16), jnp.asarray(p.T, bf16), hm)
        ctx.append((wg, bias, consts))
        xs.append(x)
        x, *kept = forward_layer(layer, x, wg, bias, qvb[:, layer], b1[layer], norm_vec[layer], consts, steps)
        saved.append(kept)
    out = both_halves(x, me)
    g = cot
    big, little = [None] * LAYERS, [None] * LAYERS
    for layer in reversed(range(LAYERS)):
        wg, bias, consts = ctx[layer]
        g, gw, gqv, gb1, ds, gnv = backward_layer(
            layer, g, xs[layer], saved[layer], wg, bias, norm_vec[layer], consts, live, steps
        )
        mine = lax.dynamic_index_in_dim(gw, me, 0, keepdims=False)
        other = lax.ppermute(lax.dynamic_index_in_dim(gw, 1 - me, 0, keepdims=False), "mp", [(0, 1), (1, 0)])
        total = (mine.astype(f32) + other.astype(f32)).astype(bf16)
        big[layer] = lax.psum_scatter(total, "dp", scatter_dimension=0, tiled=True).astype(f32)
        ds = ds.reshape(2, WROW, GROUP, WROW)[:, :WSEQ, :, :WSEQ].transpose(0, 2, 3, 1)
        gt = jnp.dot(ds.reshape(2 * GROUP, WSEQ * WSEQ), onehot.T, precision=lax.Precision.HIGHEST)
        little[layer] = jnp.concatenate([gqv.reshape(-1), gb1.reshape(-1), gt.reshape(-1), gnv[:6].reshape(-1)])
    x_grad = both_halves(g, me)
    little = lax.psum(jnp.stack(little), ("dp", "mp"))
    big = jnp.stack(big)
    one_grad = big[:, :, :FFH]
    two_grad = big[:, :, FFH:ATT].transpose(0, 2, 1)
    qkv_grad = big[:, :, ATT : ATT + QKV].reshape(LAYERS, part, 3, HALF)
    proj_grad = big[:, :, ATT + QKV :].transpose(0, 2, 1)
    cut = lambda a: lax.dynamic_index_in_dim(a, me, 1, keepdims=False)
    at = 2 * 2 * HALF
    qv_grad = cut(little[:, :at].reshape(LAYERS, 2, 2, HALF).transpose(0, 2, 1, 3))
    bias_grad = cut(little[:, at : at + 2 * FFH].reshape(LAYERS, 2, FFH))
    at += 2 * FFH
    table_grad = cut(little[:, at : at + 2 * GROUP * TABLE].reshape(LAYERS, 2, GROUP, TABLE)).transpose(0, 2, 1)
    at += 2 * GROUP * TABLE
    norm_grad = little[:, at:].reshape(LAYERS, 6, D)
    groups = [
        adam_update(w_qkv, m_qkv, v_qkv, qkv_grad, decay_rate),
        adam_update(w_proj, m_proj, v_proj, proj_grad, decay_rate),
        adam_update(w_fc_one, m_fc_one, v_fc_one, one_grad, decay_rate),
        adam_update(w_fc_two, m_fc_two, v_fc_two, two_grad, decay_rate),
        adam_update(qv_bias, m_qv_bias, v_qv_bias, qv_grad, 0.0),
        adam_update(fc_one_bias, m_fc_one_bias, v_fc_one_bias, bias_grad, 0.0),
        adam_update(rel_table, m_rel_table, v_rel_table, table_grad, 0.0),
        adam_update(norm_vec, m_norm_vec, v_norm_vec, norm_grad, 0.0),
    ]
    return (out, x_grad, *[grp[k] for k in range(3) for grp in groups])


def solution(mesh):
    params = (
        P(None, "dp", None, "mp"), P(None, "mp", "dp"), P(None, "dp", "mp"), P(None, "mp", "dp"),
        P(None, None, "mp"), P(None, "mp"), P(None, None, "mp"), P(),
    )
    act = (P("dp", None, None), P("dp", None, None))
    return jax.shard_map(
        local,
        mesh=mesh,
        in_specs=(*act, P("dp"), P(), *params, *params, *params),
        out_specs=(*act, *params, *params, *params),
        check_vma=False,
    )
```

time: 1690 us -> 742 us (0.44)
  local copies, waits for them, and re-layouts: 408 us -> 41.5 us
  blocking collectives: 242 us -> 1.99 us
  matrix products: 234 us -> 5.74 us
  waiting for transfers between devices: 638 us -> 435 us
  Pallas kernels: 0 us -> 197 us
  other arithmetic: 139 us -> 39.6 us
    dot_general x38 -> x4, matrix products: 214 us -> 5.74 us  [the longest x2 3.95 us: bias_cols(): jnp.dot(table.T, onehot, precision=lax.Precision.HIGHEST)]
    pallas_call x0 -> x4, Pallas kernels: none -> 197 us  [the longest x2 112 us: backward_layer(): pl.pallas_call(functools.partial(backward_kernel, first, last, windows, s...]
    another operation x36 -> x6, local copies, waits for them, and re-layouts: 187 us -> 1.02 us  [the longest x1 0.87 us: bias_cols(): return by_j.reshape(-1, 2, WROW, LANES)]
    all_gather x4 -> x1, blocking collectives: 169 us -> 1.99 us  [local(): small = lax.all_gather(small, 'mp')]
    reduce_scatter x8 -> x2, waiting for transfers between devices: 398 us -> 256 us  [local(): lax.psum_scatter(total, 'dp', scatter_dimension=0, tiled=True).astype(f32)]
    reduce_sum x22 -> x0, other arithmetic: 93.2 us -> none  [the longest x4 24.6 us: norm_backward(): return (grad_in, jnp.sum(grad_norm * norm_hat, 0), jnp.sum(grad_norm, 0))]
    all_gather x4 -> x1, waiting for transfers between devices: 156 us -> 74.7 us  [local(): gathered = lax.all_gather(packed, ('mp', 'dp'))]
    psum x1 -> x0, blocking collectives: 72.4 us -> none  [local(): lax.psum((stacked_small[0], stacked_small[1], stacked_small[2], norm_term...]
  transfers between devices with their start and end apart: 19 -> 8, of which waited for: 15 -> 6; matrix products, arithmetic and copies ran while one was open for 16% -> 8% of each run, Pallas kernels for 0% -> 0%
where the time goes in v1:
time: 742 us; the launch traced here: 737 us
  waiting for transfers between devices  435 us (59%)
  Pallas kernels  197 us (27%)
  local copies, waits for them, and re-layouts  41.5 us (6%)
  other arithmetic  39.6 us (5%)
  between operations  15.3 us (2%)
    reduce_scatter x2, waiting for transfers between devices, local(): lax.psum_scatter(total, 'dp', scatter_dimension=0, tiled=True).astype(f32)  256 us
    pallas_call x2, Pallas kernels, backward_layer(): pl.pallas_call(functools.partial(backward_kernel, first, last, windows, s...  112 us
    psum x1, waiting for transfers between devices, local(): little = lax.psum(jnp.stack(little), ('dp', 'mp'))  96.8 us
    pallas_call x2, Pallas kernels, forward_layer(): pl.pallas_call(functools.partial(forward_kernel, first, last, windows), n...  84.4 us
    all_gather x1, waiting for transfers between devices, local(): gathered = lax.all_gather(packed, ('mp', 'dp'))  74.7 us
  transfers between devices with their start and end apart: 8, of which 6 were waited for; matrix products, arithmetic and copies ran while one was open for 8% of the time, Pallas kernels for 0%

profile of v1, /device:TPU:0, one launch (start us, length us, event | category | flops | bytes accessed | tf_op | source)
XLA Modules:
  0.0 736.9 jit_solution(17010917028683477386)
XLA Ops:
  7.3 1.1 convert.25
  8.6 1.0 convert_bitcast_fusion
  9.6 1.0 convert_bitcast_fusion.1
  10.5 0.8 convert_bitcast_fusion.3
  11.4 0.8 pad_maximum_fusion.2
  12.2 0.8 copy.168
  13.3 2.0 all-gather.1
  16.9 2.0 fusion.11
  19.2 0.9 reshape_broadcast_in_dim.3.bias_ref
  20.1 1.0 copy.175
  21.1 2.0 fusion.14
  23.4 0.9 add.192
  24.3 1.0 add.194
  25.2 1.1 add.195
  27.0 0.8 fusion.54
  27.8 1.1 constant_dynamic-slice_fusion.2.x_ref
  29.0 3.5 constant_dynamic-slice_fusion.1.g_ref
  34.4 1.2 broadcast_add_fusion.bias_ref
  35.6 74.7 %all-gather.4.cloned.1.call-done = bf16[32,2,32,3072]{3,2,1,0:T(8,128)(2,1)} async-done(((bf16[1,2,32,3072]{3,2,1,0:T(8,128)(2,1)}), bf16[32,2,32,3072]{3,2,1,0:T(8,128)(2,1)}) %all-gather.4.cloned.1.call-update) | async-done | bytes 12582928 | tf_op jit(solution)/shard_map/all_gather | solution.py:475
  110.3 11.3 %fusion.50 = (bf16[2,16,1,32,3072]{4,3,2,1,0:T(8,128)(2,1)}, bf16[2,16,1,32,3072]{4,3,2,1,0:T(8,128)(2,1)}) fusion(bf16[2,16,2,32,3072]{4,3,2,1,0:T(8,128)(2,1)} %bitcast.168), kind=kLoop, calls=%fused_computation.95 | loop fusion | bytes 25165824 | tf_op jit(solution)/shard_map/slice | solution.py:492
  121.6 42.1 %forward_0.1 = (f32[1200,512]{1,0:T(8,128)}, f32[1200,512]{1,0:T(8,128)}, bf16[1536,1536]{1,0:T(8,128)(2,1)}, bf16[1200,512]{1,0:T(8,128)(2,1)}, bf16[1200,2048]{1,0:T(8,128)(2,1)}, /*index=5*/bf16[1200,2048]{1,0:T(8,128)(2,1)}) custom-call(bf16[6,196,512]{2,1,0:T(8,128)(2,1)} %constant_dynamic-slice_fusion.2.x_ref, bf16[2,512,3072]{2,1,0:T(8,128)(2,1)} %bitcast.164, ...), custom_call_target="tpu_custom_call" | custom-call | tf_op jit(solution)/shard_map/forward_0/pallas_call | solution.py:342
  163.7 42.3 %forward_1.1 = (f32[6,196,512]{2,1,0:T(8,128)}, f32[1200,512]{1,0:T(8,128)}, bf16[1536,1536]{1,0:T(8,128)(2,1)}, bf16[1200,512]{1,0:T(8,128)(2,1)}, bf16[1200,20...) custom-call(f32[1200,512]{1,0:T(8,128)} %get-tuple-element.50.x_ref, bf16[2,512,3072]{2,1,0:T(8,128)(2,1)} %bitcast.160, ...), custom_call_target="tpu_custom_call" | custom-call | tf_op jit(solution)/shard_map/forward_1/pallas_call | solution.py:342
  206.6 56.4 %backward_1.1 = (f32[1200,512]{1,0:T(8,128)}, bf16[2,512,3072]{2,1,0:T(8,128)(2,1)}, f32[2,512]{1,0:T(2,128)}, f32[1,2048]{1,0:T(1,128)}, f32[2,64,512]{2,1,0:T(8,128)}, /*index=5*/f32[8,512]{1,0:T(8,128)}) custom-call(f32[6,196,512]{2,1,0:T(8,128)} %constant_dynamic-slice_fusion.1.g_ref, f32[1200,512]{1,0:T(8,128)} %get-tuple-element.50.x_ref, ...), custom_call_target="tpu_custom_call" | custom-call | tf_op jit(solution)/shard_map/backward_1/pallas_call | solution.py:387
  263.0 55.9 %backward_0.1 = (f32[6,196,512]{2,1,0:T(8,128)}, bf16[2,512,3072]{2,1,0:T(8,128)(2,1)}, f32[2,512]{1,0:T(2,128)}, f32[1,2048]{1,0:T(1,128)}, f32[2,64,512]{2,1,0:T(8,128)}, /*index=5*/f32[8,512]{1,0:T(8,128)}) custom-call(f32[1200,512]{1,0:T(8,128)} %get-tuple-element.57.g_ref, bf16[6,196,512]{2,1,0:T(8,128)(2,1)} %constant_dynamic-slice_fusion.2.x_ref, ...), custom_call_target="tpu_custom_call" | custom-call | tf_op jit(solution)/shard_map/backward_0/pallas_call | solution.py:387
  319.0 3.8 dynamic-slice_bitcast_fusion.1
  323.7 0.9 fusion.8
  325.3 0.9 fusion.7
  327.3 1.6 collective-permute-done.2
  328.9 5.7 fusion.1
  334.6 2.1 dynamic-slice_bitcast_fusion
  337.1 5.4 collective-permute-done.3
  342.5 4.8 fusion
  347.4 1.6 copy-done.2
  349.5 96.8 %all-reduce.6.cloned.1.call-done = f32[2,8848]{1,0:T(2,128)} async-done(((f32[2,8848]{1,0:T(2,128)}), f32[2,8848]{1,0:T(2,128)}) %all-reduce.6.cloned.1.call-update) | async-done | bytes 70800 | tf_op jit(solution)/shard_map/psum | solution.py:517
  446.3 0.7 slice.134
  449.7 0.8 slice.135
  450.6 0.7 slice.133
  453.3 3.0 broadcast_select_fusion.1
  456.3 2.8 pad_maximum_fusion.1
  459.2 3.1 broadcast_select_fusion.3
  462.3 2.8 pad_maximum_fusion
  465.2 120.3 %reduce-scatter.3.cloned.1.call-done = bf16[32,3072]{1,0:T(8,128)(2,1)} async-done(((bf16[512,3072]{1,0:T(8,128)(2,1)}), bf16[32,3072]{1,0:T(8,128)(2,1)}) %reduce-scatter.3.cloned.1.call-update) | async-done | bytes 196624 | tf_op jit(solution)/shard_map/reduce_scatter | solution.py:512
  585.4 136.0 %reduce-scatter.5.cloned.1.call-done = bf16[32,3072]{1,0:T(8,128)(2,1)} async-done(((bf16[512,3072]{1,0:T(8,128)(2,1)}), bf16[32,3072]{1,0:T(8,128)(2,1)}) %reduce-scatter.5.cloned.1.call-update) | async-done | bytes 196624 | tf_op jit(solution)/shard_map/reduce_scatter | solution.py:512
  721.5 1.2 maximum_convert_fusion
  722.7 1.6 multiply_subtract_fusion.3
  724.3 1.9 multiply_subtract_fusion
  726.2 2.0 multiply_subtract_fusion.1
  728.3 1.9 multiply_subtract_fusion.2
  (136 shorter events, 13.4 us)
Async XLA Ops:
  7.2 20.6 %copy-start = (bf16[12,196,512]{2,1,0:T(8,128)(2,1)S(1)}, bf16[12,196,512]{2,1,0:T(8,128)(2,1)}, u32[]{:S(2)}) copy-start(bf16[12,196,512]{2,1,0:T(8,128)(2,1)} %param.34) | copy-start | bytes 7225348
  7.2 6.0 copy-start.24
  7.2 6.0 copy-start.14
  7.2 9.7 %copy-start.16 = (s32[49,49]{1,0:T(8,128)S(1)}, s32[49,49]{1,0:T(8,128)}, u32[]{:S(2)}) copy-start(s32[49,49]{1,0:T(8,128)} %param.37) | copy-start | bytes 28816
  7.3 103.0 %all-gather.4.cloned.1.call-start = ((), (), s32[]{:S(2)}) async-start(), calls=%async_computation.2 | async-start | bytes 12976128 | tf_op jit(solution)/shard_map/all_gather | solution.py:475
  12.2 434.1 %all-reduce.6.cloned.1.call-start = ((), (), s32[]{:S(2)}) async-start(), calls=%async_computation.5 | async-start | bytes 143360 | tf_op jit(solution)/shard_map/psum | solution.py:517
  27.8 5.9 copy-start.12
  29.0 5.4 copy-start.3
  29.0 5.4 copy-start.4
  319.0 4.2 copy-start.17
  319.0 4.3 copy-start.10
  319.0 5.7 copy-start.23
  319.0 5.7 copy-start.33
  319.0 5.7 copy-start.29
  319.0 5.8 copy-start.9
  322.9 3.4 copy-start.22
  322.9 3.5 copy-start.32
  322.9 3.5 copy-start.28
  322.9 6.0 collective-permute-start.2
  327.2 258.2 %reduce-scatter.3.cloned.1.call-start = ((), (), s32[]{:S(2)}) async-start(), calls=%async_computation.3 | async-start | bytes 3342336 | tf_op jit(solution)/shard_map/reduce_scatter | solution.py:512
  334.6 386.9 %reduce-scatter.5.cloned.1.call-start = ((), (), s32[]{:S(2)}) async-start(), calls=%async_computation.4 | async-start | bytes 3342336 | tf_op jit(solution)/shard_map/reduce_scatter | solution.py:512
  336.8 5.7 collective-permute-start.3
  347.3 1.7 copy-start.2
  347.3 100.6 %copy-start.25 = (f32[2,2,256]{2,1,0:T(2,128)S(1)}, f32[2,2,256]{2,1,0:T(2,128)}, u32[]{:S(2)}) copy-start(f32[2,2,256]{2,1,0:T(2,128)} %param.42) | copy-start | bytes 12292
  347.3 100.6 %copy-start.30 = (f32[2,2,256]{2,1,0:T(2,128)S(1)}, f32[2,2,256]{2,1,0:T(2,128)}, u32[]{:S(2)}) copy-start(f32[2,2,256]{2,1,0:T(2,128)} %param.50) | copy-start | bytes 12292
  347.3 100.6 %copy-start.31 = (f32[2,2,256]{2,1,0:T(2,128)S(1)}, f32[2,2,256]{2,1,0:T(2,128)}, u32[]{:S(2)}) copy-start(f32[2,2,256]{2,1,0:T(2,128)} %param.58) | copy-start | bytes 12292
  347.3 104.0 %copy-start.15 = (f32[2,1024]{1,0:T(2,128)S(1)}, f32[2,1024]{1,0:T(2,128)}, u32[]{:S(2)}) copy-start(f32[2,1024]{1,0:T(2,128)} %param.43) | copy-start | bytes 24580
  347.3 104.0 %copy-start.26 = (f32[2,1024]{1,0:T(2,128)S(1)}, f32[2,1024]{1,0:T(2,128)}, u32[]{:S(2)}) copy-start(f32[2,1024]{1,0:T(2,128)} %param.51) | copy-start | bytes 24580
  347.3 104.0 %copy-start.27 = (f32[2,1024]{1,0:T(2,128)S(1)}, f32[2,1024]{1,0:T(2,128)}, u32[]{:S(2)}) copy-start(f32[2,1024]{1,0:T(2,128)} %param.59) | copy-start | bytes 24580
  347.3 104.6 %copy-start.13 = (f32[2,169,8]{1,2,0:T(8,128)S(1)}, f32[2,169,8]{1,2,0:T(8,128)}, u32[]{:S(2)}) copy-start(f32[2,169,8]{1,2,0:T(8,128)} %param.44) | copy-start | bytes 32452
  347.3 104.6 %copy-start.20 = (f32[2,169,8]{1,2,0:T(8,128)S(1)}, f32[2,169,8]{1,2,0:T(8,128)}, u32[]{:S(2)}) copy-start(f32[2,169,8]{1,2,0:T(8,128)} %param.52) | copy-start | bytes 32452
  347.3 104.6 %copy-start.21 = (f32[2,169,8]{1,2,0:T(8,128)S(1)}, f32[2,169,8]{1,2,0:T(8,128)}, u32[]{:S(2)}) copy-start(f32[2,169,8]{1,2,0:T(8,128)} %param.60) | copy-start | bytes 32452
  347.4 105.2 %copy-start.18 = (f32[2,6,512]{2,0,1:T(2,128)S(1)}, f32[2,6,512]{2,0,1:T(2,128)}, u32[]{:S(2)}) copy-start(f32[2,6,512]{2,0,1:T(2,128)} %param.53) | copy-start | bytes 73732
  347.4 105.2 %copy-start.19 = (f32[2,6,512]{2,0,1:T(2,128)S(1)}, f32[2,6,512]{2,0,1:T(2,128)}, u32[]{:S(2)}) copy-start(f32[2,6,512]{2,0,1:T(2,128)} %param.61) | copy-start | bytes 73732
  349.0 104.3 %collective-permute-start.1 = (f32[6,196,512]{2,1,0:T(8,128)S(1)}, f32[6,196,512]{2,1,0:T(8,128)}, u32[]{:S(2)}, u32[]{:S(2)}) collective-permute-start(f32[6,196,512]{2,1,0:T(8,128)S(1)} %copy-done.2), channel_id=1, source_target_pairs={{0,1},{1,0},{2,3},{3,2},{4,5},{5,4},{6,7},{7,6},{8,9},{9,8},{10,11... | collective-permute-start | bytes 7225352 | tf_op jit(solution)/shard_map/ppermute | solution.py:450
  349.2 109.9 %collective-permute-start = (f32[6,196,512]{2,1,0:T(8,128)}, f32[6,196,512]{2,1,0:T(8,128)}, u32[]{:S(2)}, u32[]{:S(2)}) collective-permute-start(f32[6,196,512]{2,1,0:T(8,128)} %get-tuple-element.51), channel_id=1, source_target_pairs={{0,1},{1,0},{2,3},{3,2},{4,5},{5,4},{6,7},{7,6},{8,9},{9,8},{10,11... | collective-permute-start | bytes 7225352 | tf_op jit(solution)/shard_map/ppermute | solution.py:450
  462.3 260.4 %copy-start.11 = (f32[2,256,32]{1,2,0:T(8,128)S(1)}, f32[2,256,32]{1,2,0:T(8,128)}, u32[]{:S(2)}) copy-start(f32[2,256,32]{1,2,0:T(8,128)} %param.39) | copy-start | bytes 196612
  462.3 262.0 %copy-start.5 = (f32[2,1024,32]{1,2,0:T(8,128)S(1)}, f32[2,1024,32]{1,2,0:T(8,128)}, u32[]{:S(2)}) copy-start(f32[2,1024,32]{1,2,0:T(8,128)} %param.41) | copy-start | bytes 786436
  462.3 262.0 %copy-start.8 = (f32[2,1024,32]{1,2,0:T(8,128)S(1)}, f32[2,1024,32]{1,2,0:T(8,128)}, u32[]{:S(2)}) copy-start(f32[2,1024,32]{1,2,0:T(8,128)} %param.49) | copy-start | bytes 786436
  465.1 261.1 %copy-start.6 = (f32[2,32,1024]{2,1,0:T(8,128)S(1)}, f32[2,32,1024]{2,1,0:T(8,128)}, u32[]{:S(2)}) copy-start(f32[2,32,1024]{2,1,0:T(8,128)} %param.40) | copy-start | bytes 786436
  465.1 263.1 %copy-start.7 = (f32[2,32,3,256]{3,1,2,0:T(8,128)S(1)}, f32[2,32,3,256]{3,1,2,0:T(8,128)}, u32[]{:S(2)}) copy-start(f32[2,32,3,256]{3,1,2,0:T(8,128)} %param.38) | copy-start | bytes 589828
  721.5 8.7 %copy-start.1 = (bf16[12,196,512]{2,1,0:T(8,128)(2,1)S(1)}, bf16[12,196,512]{2,1,0:T(8,128)(2,1)}, u32[]{:S(2)}) copy-start(bf16[12,196,512]{2,1,0:T(8,128)(2,1)} %param.34) | copy-start | bytes 7225348
Sparse Core Ops, SparseCore 0:
  12.3 97.8 all-gather.3
  327.3 118.9 all-reduce.5
  451.3 134.0 reduce-scatter.2
  590.3 131.1 reduce-scatter.4

commit v2 on v1

--- a/solution.py
+++ b/solution.py
@@ -436,6 +436,397 @@
         by_j = by_j[None]
     return by_j.reshape(-1, 2, WROW, LANES)
 
+NZ, NY, NX = 4, 2, 2
+PEERS = NZ * NY * NX
+MESH_ID = pl.DeviceIdType.MESH
+
+
+class Place:
+    def __init__(self):
+        d = lax.axis_index("dp")
+        self.d, self.m = d, lax.axis_index("mp")
+        self.z, self.y, self.x = d // 4, lax.rem(d // 2, 2), lax.rem(d, 2)
+
+    def chip(self, z, y, x):
+        return (z * NY + y) * NX + x
+
+    def at(self, dz=0, y=None, x=None, m=None):
+        y = self.y if y is None else y
+        x = self.x if x is None else x
+        return (self.chip(self.z + dz, y, x), self.m if m is None else m)
+
+    def xn(self):
+        return self.at(x=1 - self.x)
+
+    def yn(self):
+        return self.at(y=1 - self.y)
+
+    def core(self):
+        return self.at(m=1 - self.m)
+
+    def zn(self, step):
+        return self.at(dz=step)
+
+    def has(self, step):
+        return self.z < NZ - 1 if step > 0 else self.z > 0
+
+
+def remote(src, dst, send, recv, to):
+    return pltpu.make_async_remote_copy(
+        src_ref=src, dst_ref=dst, send_sem=send, recv_sem=recv, device_id=to, device_id_type=MESH_ID
+    )
+
+
+def neighbour_barrier(p, far=False):
+    sem = pltpu.get_barrier_semaphore()
+
+    def tell(to):
+        pl.semaphore_signal(sem, inc=1, device_id=to, device_id_type=MESH_ID)
+
+    for to in (p.xn(), p.yn(), p.core()):
+        tell(to)
+    count = 3
+    for step in (1, -1):
+        pl.when(p.has(step))(lambda step=step: tell(p.zn(step)))
+        count = count + p.has(step).astype(jnp.int32)
+    if far:
+        tell((p.chip((p.z + 2) % NZ, p.y, p.x), p.m))
+        count = count + 1
+    pl.semaphore_wait(sem, count)
+
+
+class Gather:
+    SEMS = 52
+    BASE = {"z": 0, "xa": 8, "yb": 12, "ya0": 16, "ya1": 20, "xb0": 24, "xb1": 28,
+            "own": 32, "ax": 36, "by": 40, "ar": 44, "br": 48}
+
+    def __init__(self, own, full, send, recv, local, lo, hi):
+        self.p, self.own, self.full = Place(), own, full
+        self.send, self.recv, self.local = send, recv, local
+        mid = (lo + hi) // 2
+        self.all, self.a, self.b = pl.ds(lo, hi - lo), pl.ds(lo, mid - lo), pl.ds(mid, hi - mid)
+
+    def region(self, kind, k, arrived):
+        p = self.p
+        oy, ox = 1 - p.y, 1 - p.x
+        if kind == "z":
+            return (p.m, k, p.y, p.x), self.all, None
+        if kind == "xa":
+            return (p.m, k, p.y, ox if arrived else p.x), self.a, p.xn()
+        if kind == "yb":
+            return (p.m, k, oy if arrived else p.y, p.x), self.b, p.yn()
+        if kind in ("ya0", "ya1"):
+            return (p.m, k, oy if arrived else p.y, p.x if kind == "ya0" else ox), self.a, p.yn()
+        if kind in ("xb0", "xb1"):
+            return (p.m, k, p.y if kind == "xb0" else oy, ox if arrived else p.x), self.b, p.xn()
+        m = 1 - p.m if arrived else p.m
+        if kind == "own":
+            return (m, k, p.y, p.x), self.all, p.core()
+        if kind == "ax":
+            return (m, k, p.y, ox), self.a, p.core()
+        if kind == "by":
+            return (m, k, oy, p.x), self.b, p.core()
+        if kind == "ar":
+            return (m, k, oy, slice(None)), self.a, p.core()
+        return (m, k, slice(None), ox), self.b, p.core()
+
+    def copy(self, kind, k, own=False, arrived=False, step=0):
+        at, cols, to = self.region(kind, k, arrived)
+        dst = self.full.at[(*at, slice(None), cols)]
+        src = self.own.at[:, cols] if own else dst
+        s = self.BASE[kind] + k
+        r = s
+        if kind == "z":
+            to = self.p.zn(step)
+            s = s + (4 if step < 0 else 0)
+        return remote(src, dst, self.send.at[s], self.recv.at[r], to)
+
+    def keep(self):
+        p = self.p
+        return pltpu.make_async_copy(
+            self.own.at[:, self.all], self.full.at[p.m, p.z, p.y, p.x, :, self.all], self.local.at[0]
+        )
+
+    def fan(self, k, own=False):
+        for kind in ("xa", "yb", "ya0", "xb0", "own"):
+            self.copy(kind, k, own).start()
+
+    def stage(self, n):
+        p = self.p
+        if n == 0:
+            self.keep().start()
+            for step in (1, -1):
+                pl.when(p.has(step))(lambda step=step: self.copy("z", p.z, True, step=step).start())
+            self.fan(p.z, True)
+        elif n <= 3:
+            for step in (1, -1):
+                k = p.z - step * n
+                inside = k >= 0 if step > 0 else k < NZ
+
+                @pl.when(inside)
+                def _():
+                    self.copy("z", k, arrived=True, step=step).wait_recv()
+                    pl.when(p.has(step))(lambda: self.copy("z", k, step=step).start())
+                    self.fan(k)
+        elif n == 4:
+            for k in range(NZ):
+                self.copy("xa", k, arrived=True).wait_recv()
+                for kind in ("ya1", "ax"):
+                    self.copy(kind, k).start()
+                self.copy("yb", k, arrived=True).wait_recv()
+                for kind in ("xb1", "by"):
+                    self.copy(kind, k).start()
+        elif n == 5:
+            for k in range(NZ):
+                for kind, rest in (("ya", "ar"), ("xb", "br")):
+                    for rel in ("0", "1"):
+                        self.copy(kind + rel, k, arrived=True).wait_recv()
+                    self.copy(rest, k).start()
+        else:
+            for k in range(NZ):
+                for kind in ("own", "ax", "by", "ar", "br"):
+                    self.copy(kind, k, arrived=True).wait_recv()
+                for kind in self.BASE:
+                    if kind != "z":
+                        self.copy(kind, k).wait_send()
+                pl.when((k <= p.z) & p.has(1))(lambda: self.copy("z", k, step=1).wait_send())
+                pl.when((k >= p.z) & p.has(-1))(lambda: self.copy("z", k, step=-1).wait_send())
+            self.keep().wait()
+
+    STAGES = 7
+
+
+def add_into(ref, at, other):
+    ref[at] = (ref[at].astype(f32) + other.astype(f32)).astype(bf16)
+
+
+class Scatter:
+    SEMS = 32
+    LOCAL = 4
+    BASE = {"core": 0, "ya": 4, "xb": 8, "xa": 12, "yb": 16, "up": 20, "down": 24}
+
+    @staticmethod
+    def scratch(rows, cols):
+        half = cols // 2
+        return [
+            pltpu.VMEM((NZ, NY, NX, rows, cols), bf16), pltpu.VMEM((NZ, NY, NX, rows, cols), bf16),
+            pltpu.VMEM((NZ, NX, rows, half), bf16), pltpu.VMEM((NZ, NY, rows, half), bf16),
+            pltpu.VMEM((NZ, rows, half), bf16), pltpu.VMEM((NZ, rows, half), bf16),
+            pltpu.VMEM((NZ, rows, cols), bf16), pltpu.VMEM((NZ, rows, cols), bf16),
+            pltpu.SemaphoreType.DMA((Scatter.SEMS,)), pltpu.SemaphoreType.DMA((Scatter.SEMS,)),
+            pltpu.SemaphoreType.DMA((Scatter.LOCAL,)),
+        ]
+
+    def __init__(self, grad, part, other, ya, xb, xa, yb, up, down, send, recv, local):
+        self.p, self.grad, self.part, self.other = Place(), grad, part, other
+        self.land = {"ya": ya, "xb": xb, "xa": xa, "yb": yb, "up": up, "down": down}
+        self.send, self.recv, self.local = send, recv, local
+        half = part.shape[-1] // 2
+        self.a, self.b = pl.ds(0, half), pl.ds(half, half)
+
+    def copy(self, kind, k):
+        p = self.p
+        oy, ox = 1 - p.y, 1 - p.x
+        full = slice(None)
+        if kind == "core":
+            src, dst, to = self.grad.at[1 - p.m, k], self.other.at[k], p.core()
+        else:
+            at, to = {
+                "ya": ((k, oy, full, full, self.a), p.yn()),
+                "xb": ((k, full, ox, full, self.b), p.xn()),
+                "xa": ((k, p.y, ox, full, self.a), p.xn()),
+                "yb": ((k, oy, p.x, full, self.b), p.yn()),
+                "up": ((k, p.y, p.x, full, full), p.zn(1)),
+                "down": ((k, p.y, p.x, full, full), p.zn(-1)),
+            }[kind]
+            src, dst = self.part.at[at], self.land[kind].at[k]
+        s = self.BASE[kind] + k
+        return remote(src, dst, self.send.at[s], self.recv.at[s], to)
+
+    def load(self, k):
+        return pltpu.make_async_copy(self.grad.at[self.p.m, k], self.part.at[k], self.local.at[k])
+
+    def pass_on(self, step):
+        p = self.p
+        kind = "up" if step > 0 else "down"
+        for dist in range(NZ - 1, 0, -1):
+            k = p.z + step * dist
+
+            @pl.when((k < NZ) & (k >= 0))
+            def _():
+                @pl.when(p.has(-step))
+                def _():
+                    self.copy(kind, k).wait_recv()
+                    add_into(self.part, (k, p.y, p.x), self.land[kind][k])
+
+                self.copy(kind, k).start()
+
+    def stage(self, n):
+        p = self.p
+        oy, ox = 1 - p.y, 1 - p.x
+        if n == 0:
+            for k in range(NZ):
+                self.copy("core", k).start()
+                self.load(k).start()
+        elif n == 1:
+            for k in range(NZ):
+                self.load(k).wait()
+                self.copy("core", k).wait_recv()
+                for y in range(NY):
+                    for x in range(NX):
+                        add_into(self.part, (k, y, x), self.other[k, y, x])
+                self.copy("ya", k).start()
+                self.copy("xb", k).start()
+        elif n == 2:
+            for k in range(NZ):
+                self.copy("ya", k).wait_recv()
+                for x in range(NX):
+                    add_into(self.part, (k, p.y, x, slice(None), self.a), self.land["ya"][k, x])
+                self.copy("xa", k).start()
+                self.copy("xb", k).wait_recv()
+                for y in range(NY):
+                    add_into(self.part, (k, y, p.x, slice(None), self.b), self.land["xb"][k, y])
+                self.copy("yb", k).start()
+        elif n == 3:
+            for k in range(NZ):
+                self.copy("xa", k).wait_recv()
+                add_into(self.part, (k, p.y, p.x, slice(None), self.a), self.land["xa"][k])
+                self.copy("yb", k).wait_recv()
+                add_into(self.part, (k, p.y, p.x, slice(None), self.b), self.land["yb"][k])
+            pl.when(p.z == 0)(lambda: self.pass_on(1))
+            pl.when(p.z == NZ - 1)(lambda: self.pass_on(-1))
+        elif n in (4, 5):
+            j = n - 3
+            pl.when(p.z == j)(lambda: self.pass_on(1))
+            pl.when(p.z == NZ - 1 - j)(lambda: self.pass_on(-1))
+        else:
+            for k in range(NZ):
+                for kind in ("core", "ya", "xb", "xa", "yb"):
+                    self.copy(kind, k).wait_send()
+                pl.when(k > p.z)(lambda: self.copy("up", k).wait_send())
+                pl.when(k < p.z)(lambda: self.copy("down", k).wait_send())
+
+    STAGES = 7
+
+    def result(self, out):
+        p = self.p
+        out[...] = self.part[p.z, p.y, p.x].astype(f32)
+        for step, kind in ((1, "up"), (-1, "down")):
+
+            @pl.when(p.has(-step))
+            def _():
+                self.copy(kind, p.z).wait_recv()
+                out[...] += self.land[kind][p.z].astype(f32)
+
+
+class Total:
+    STEPS = 5
+
+    @staticmethod
+    def scratch(shape):
+        return [
+            pltpu.VMEM((Total.STEPS, *shape), f32), pltpu.VMEM((Total.STEPS, *shape), f32),
+            pltpu.SemaphoreType.DMA((Total.STEPS,)), pltpu.SemaphoreType.DMA((Total.STEPS,)),
+        ]
+
+    def __init__(self, start, held, land, send, recv):
+        self.p, self.start, self.held, self.land, self.send, self.recv = Place(), start, held, land, send, recv
+
+    def copy(self, n):
+        p = self.p
+        pair = p.z + 1 - 2 * lax.rem(p.z, 2)
+        far = lax.rem(p.z + 2, NZ)
+        to = (p.core(), p.yn(), p.xn(), (p.chip(pair, p.y, p.x), p.m), (p.chip(far, p.y, p.x), p.m))[n]
+        src = self.start if n == 0 else self.held.at[n - 1]
+        return remote(src, self.land.at[n], self.send.at[n], self.recv.at[n], to)
+
+    def stage(self, n):
+        if n > 0:
+            self.copy(n - 1).wait_recv()
+            before = self.start[...] if n == 1 else self.held[n - 2]
+            self.held[n - 1] = before + self.land[n - 1]
+        if n < self.STEPS:
+            self.copy(n).start()
+        else:
+            for k in range(self.STEPS):
+                self.copy(k).wait_send()
+
+
+def gather_kernel(own_ref, small_ref, full_a, full_b, both_ref, send, recv, local, ssend, srecv):
+    p = Place()
+    neighbour_barrier(p)
+    swap = remote(small_ref, both_ref.at[p.m], ssend.at[0], srecv.at[0], p.core())
+    swap.start()
+    cols = own_ref.shape[-1]
+    parts = []
+    for layer, full in enumerate((full_a, full_b)):
+        for lo, hi in ((ATT, COLS), (0, ATT)):
+            n = len(parts)
+            if cols != COLS:
+                lo, hi = lo * cols // COLS, hi * cols // COLS
+            parts.append(Gather(own_ref.at[layer], full, send.at[n], recv.at[n], local.at[n], lo, hi))
+    for n in range(Gather.STAGES):
+        for g in parts:
+            g.stage(n)
+    both_ref[p.m] = small_ref[...]
+    swap.wait()
+
+
+def gather_all(packed, small):
+    rows, cols = packed.shape[1:]
+    full = jax.ShapeDtypeStruct((2, NZ, NY, NX, rows, cols), bf16)
+    n = 2 * LAYERS
+    return pl.pallas_call(
+        gather_kernel,
+        name="gather",
+        out_shape=[full, full, jax.ShapeDtypeStruct((2, *small.shape), f32)],
+        in_specs=[pl.BlockSpec(memory_space=pltpu.VMEM)] * 2,
+        out_specs=[pl.BlockSpec(memory_space=pl.ANY)] * 2 + [pl.BlockSpec(memory_space=pltpu.VMEM)],
+        scratch_shapes=[
+            pltpu.SemaphoreType.DMA((n, Gather.SEMS)), pltpu.SemaphoreType.DMA((n, Gather.SEMS)),
+            pltpu.SemaphoreType.DMA((n, 1)), pltpu.SemaphoreType.DMA((1,)), pltpu.SemaphoreType.DMA((1,)),
+        ],
+        compiler_params=pltpu.CompilerParams(collective_id=1, has_side_effects=True),
+    )(packed, small)
+
+
+def scatter_kernel(with_small, grad_ref, *refs):
+    if with_small:
+        small_ref, out_ref, small_out, *rest = refs
+        total = Total(small_ref, *rest[-4:])
+        rest = rest[:-4]
+    else:
+        out_ref, *rest = refs
+    p = Place()
+    neighbour_barrier(p, far=with_small)
+    s = Scatter(grad_ref, *rest)
+    for n in range(Scatter.STAGES - 1):
+        s.stage(n)
+        if with_small:
+            total.stage(n)
+    s.result(out_ref)
+    s.stage(Scatter.STAGES - 1)
+    if with_small:
+        small_out[...] = total.held[Total.STEPS - 1]
+
+
+def scatter_sum(grad, small, ident):
+    rows, cols = grad.shape[-2:]
+    with_small = small is not None
+    vm = pl.BlockSpec(memory_space=pltpu.VMEM)
+    out = [jax.ShapeDtypeStruct((rows, cols), f32)]
+    if with_small:
+        out.append(jax.ShapeDtypeStruct(small.shape, f32))
+    return pl.pallas_call(
+        functools.partial(scatter_kernel, with_small),
+        name=f"scatter_{ident}",
+        out_shape=out,
+        in_specs=[pl.BlockSpec(memory_space=pl.ANY)] + [vm] * with_small,
+        out_specs=[vm] * len(out),
+        scratch_shapes=Scatter.scratch(rows, cols) + (Total.scratch(small.shape) if with_small else []),
+        compiler_params=pltpu.CompilerParams(collective_id=ident, has_side_effects=True, vmem_limit_bytes=VLIM),
+    )(*((grad, small) if with_small else (grad,)))
+
 
 def adam_update(weight_in, moment_one, moment_two, grad_sum, decay):
     new_one = beta_one * moment_one + (1.0 - beta_one) * grad_sum
@@ -453,8 +844,17 @@
     return jnp.concatenate([low, high], 0)
 
 
+SMALL = 2 * HALF + FFH + TABLE * GROUP
+LITTLE = 4 * HALF + 2 * FFH + 2 * GROUP * TABLE + 6 * D
+
+
+def lanes_of(a):
+    flat = a.reshape(-1)
+    return jnp.pad(flat, (0, -flat.size % 1024)).reshape(-1, 128)
+
+
 def local(
-    tokens, cotangent, image_count, rel_index,
+    fast, tokens, cotangent, image_count, rel_index,
     w_qkv, w_proj, w_fc_one, w_fc_two, qv_bias, fc_one_bias, rel_table, norm_vec,
     m_qkv, m_proj, m_fc_one, m_fc_two, m_qv_bias, m_fc_one_bias, m_rel_table, m_norm_vec,
     v_qkv, v_proj, v_fc_one, v_fc_two, v_qv_bias, v_fc_one_bias, v_rel_table, v_norm_vec,
@@ -472,11 +872,17 @@
     packed = jnp.concatenate(
         [w_fc_one, w_fc_two.transpose(0, 2, 1), w_qkv.reshape(LAYERS, part, QKV), w_proj.transpose(0, 2, 1)], 2
     ).astype(bf16)
-    gathered = lax.all_gather(packed, ("mp", "dp"))
     small = jnp.concatenate(
         [qv_bias.reshape(LAYERS, -1), fc_one_bias, rel_table.reshape(LAYERS, -1)], 1
     )
-    small = lax.all_gather(small, "mp")
+    if fast:
+        *weights, small = gather_all(packed, lanes_of(small))
+        weights = [w.reshape(2, D, COLS) for w in weights]
+        small = small.reshape(2, -1)[:, : LAYERS * SMALL].reshape(2, LAYERS, SMALL)
+    else:
+        weights = lax.all_gather(packed, ("mp", "dp")).reshape(2, -1, LAYERS, part, COLS)
+        weights = [weights[:, :, layer].reshape(2, D, COLS) for layer in range(LAYERS)]
+        small = lax.all_gather(small, "mp")
     qvb = small[:, :, : 2 * HALF].reshape(2, LAYERS, 2, HALF)
     b1 = small[:, :, 2 * HALF : 2 * HALF + FFH].transpose(1, 0, 2).reshape(LAYERS, 1, 2 * FFH)
     table = small[:, :, 2 * HALF + FFH :].reshape(2, LAYERS, TABLE, GROUP).transpose(1, 2, 0, 3)
@@ -489,8 +895,7 @@
     for layer in range(LAYERS):
         shifted = layer % 2 == 1
 
-        wg = gathered.reshape(2, -1, LAYERS, part, COLS)[:, :, layer]
-        wg = wg.reshape(2, D, COLS)
+        wg = weights[layer]
         bias = bias_cols(onehot, table[layer], shifted)
         p = permutation(shifted)
         consts = (jnp.asarray(p, bf16), jnp.asarray(p.T, bf16), hm)
@@ -506,15 +911,24 @@
         g, gw, gqv, gb1, ds, gnv = backward_layer(
             layer, g, xs[layer], saved[layer], wg, bias, norm_vec[layer], consts, live, steps
         )
+        ds = ds.reshape(2, WROW, GROUP, WROW)[:, :WSEQ, :, :WSEQ].transpose(0, 2, 3, 1)
+        gt = jnp.dot(ds.reshape(2 * GROUP, WSEQ * WSEQ), onehot.T, precision=lax.Precision.HIGHEST)
+        little[layer] = jnp.concatenate([gqv.reshape(-1), gb1.reshape(-1), gt.reshape(-1), gnv[:6].reshape(-1)])
+        if fast:
+            gw = gw.reshape(2, NZ, NY, NX, part, COLS)
+            if layer > 0:
+                (big[layer],) = scatter_sum(gw, None, 2 + layer)
+            else:
+                big[layer], total = scatter_sum(gw, lanes_of(jnp.stack(little)), 2 + layer)
+                little = total.reshape(-1)[: LAYERS * LITTLE].reshape(LAYERS, LITTLE)
+            continue
         mine = lax.dynamic_index_in_dim(gw, me, 0, keepdims=False)
         other = lax.ppermute(lax.dynamic_index_in_dim(gw, 1 - me, 0, keepdims=False), "mp", [(0, 1), (1, 0)])
         total = (mine.astype(f32) + other.astype(f32)).astype(bf16)
         big[layer] = lax.psum_scatter(total, "dp", scatter_dimension=0, tiled=True).astype(f32)
-        ds = ds.reshape(2, WROW, GROUP, WROW)[:, :WSEQ, :, :WSEQ].transpose(0, 2, 3, 1)
-        gt = jnp.dot(ds.reshape(2 * GROUP, WSEQ * WSEQ), onehot.T, precision=lax.Precision.HIGHEST)
-        little[layer] = jnp.concatenate([gqv.reshape(-1), gb1.reshape(-1), gt.reshape(-1), gnv[:6].reshape(-1)])
     x_grad = both_halves(g, me)
-    little = lax.psum(jnp.stack(little), ("dp", "mp"))
+    if not fast:
+        little = lax.psum(jnp.stack(little), ("dp", "mp"))
     big = jnp.stack(big)
     one_grad = big[:, :, :FFH]
     two_grad = big[:, :, FFH:ATT].transpose(0, 2, 1)
@@ -548,7 +962,7 @@
     )
     act = (P("dp", None, None), P("dp", None, None))
     return jax.shard_map(
-        local,
+        functools.partial(local, mesh.shape["dp"] == PEERS),
         mesh=mesh,
         in_specs=(*act, P("dp"), P(), *params, *params, *params),
         out_specs=(*act, *params, *params, *params),

time: 742 us -> 436 us (0.59)
  waiting for transfers between devices: 435 us -> 0.01 us
  Pallas kernels: 197 us -> 368 us
  local copies, waits for them, and re-layouts: 41.5 us -> 25.3 us
  between operations: 15.3 us -> 2.45 us
  other arithmetic: 39.6 us -> 27.4 us
    reduce_scatter x2 -> x0, waiting for transfers between devices: 256 us -> none  [local(): lax.psum_scatter(total, 'dp', scatter_dimension=0, tiled=True).astype(f32)]
    pallas_call x0 -> x3, Pallas kernels: none -> 171 us  [the longest x2 108 us: scatter_sum(): pl.pallas_call(functools.partial(scatter_kernel, with_small), name=f'scat...]
    psum x1 -> x0, waiting for transfers between devices: 96.8 us -> none  [local(): little = lax.psum(jnp.stack(little), ('dp', 'mp'))]
    all_gather x1 -> x0, waiting for transfers between devices: 74.7 us -> none  [local(): gathered = lax.all_gather(packed, ('mp', 'dp'))]
    slice x2 -> x1, local copies, waits for them, and re-layouts: 11.4 us -> 0.01 us  [local(): small = small.reshape(2, -1)[:, :LAYERS * SMALL].reshape(2, LAYERS, SMALL)]
    convert_element_type x2 -> x0, other arithmetic: 10.5 us -> none  [local(): total = (mine.astype(f32) + other.astype(f32)).astype(bf16)]
  transfers between devices with their start and end apart: 8 -> 2, of which waited for: 6 -> 0; matrix products, arithmetic and copies ran while one was open for 8% -> 6% of each run, Pallas kernels for 0% -> 25%
where the time goes in v2:
time: 436 us; the launch traced here: 429 us
  Pallas kernels  368 us (84%)
  other arithmetic  27.4 us (6%)
  local copies, waits for them, and re-layouts  25.3 us (6%)
  matrix products  5.74 us (1%)
    pallas_call x2, Pallas kernels, backward_layer(): pl.pallas_call(functools.partial(backward_kernel, first, last, windows, s...  112 us
    pallas_call x2, Pallas kernels, scatter_sum(): pl.pallas_call(functools.partial(scatter_kernel, with_small), name=f'scat...  108 us
    pallas_call x2, Pallas kernels, forward_layer(): pl.pallas_call(functools.partial(forward_kernel, first, last, windows), n...  84.9 us
    pallas_call x1, Pallas kernels, gather_all(): pl.pallas_call(gather_kernel, name='gather', out_shape=[full, full, jax.S...  62.5 us
    sub x8, other arithmetic, adam_update(): weight_in - learn_rate * (hat_one / (jnp.sqrt(hat_two) + adam_eps) + deca...  9.73 us
  transfers between devices with their start and end apart: 2, of which 0 were waited for; matrix products, arithmetic and copies ran while one was open for 6% of the time, Pallas kernels for 25%

profile of v2, /device:TPU:0, one launch (start us, length us, event | category | flops | bytes accessed | tf_op | source)
XLA Modules:
  0.0 429.4 jit_solution(16939514262298747287)
XLA Ops:
  0.7 1.1 convert_bitcast_fusion.1
  1.8 1.0 convert.15
  2.8 1.0 convert_bitcast_fusion
  3.8 0.8 convert_bitcast_fusion.2
  4.6 0.8 copy.131
  5.6 0.7 copy.168
  6.3 0.7 pad_maximum_fusion.5
  7.7 0.8 pad_maximum_fusion.2.own_ref
  8.5 62.5 %gather.1 = (bf16[2,4,2,2,32,3072]{5,4,3,2,1,0:T(8,128)(2,1)}, bf16[2,4,2,2,32,3072]{5,4,3,2,1,0:T(8,128)(2,1)}, f32[2,48,128]{2,1,0:T(8,128)}) custom-call(bf16[2,32,3072]{2,1,0:T(8,128)(2,1)} %pad_maximum_fusion.2.own_ref, f32[48,128]{1,0:T(8,128)} %pad_bitcast_fusion.1.small_ref), custom_call_target="tpu_custom_call" | custom-call | tf_op jit(solution)/shard_map/gather/pallas_call | solution.py:779
  71.0 0.8 copy.194
  72.9 0.7 fusion.50
  73.7 2.0 fusion.9
  76.0 0.9 reshape_broadcast_in_dim.3.bias_ref
  77.5 1.0 copy.137
  78.5 2.0 fusion.12
  80.8 0.9 add.176
  81.7 1.0 add.178
  82.7 1.1 add.179
  83.7 1.2 constant_dynamic-slice_fusion.2.x_ref
  84.9 3.5 constant_dynamic-slice_fusion.1.g_ref
  89.7 1.1 broadcast_add_fusion.bias_ref
  90.8 42.6 %forward_0.1 = (f32[1200,512]{1,0:T(8,128)}, f32[1200,512]{1,0:T(8,128)}, bf16[1536,1536]{1,0:T(8,128)(2,1)}, bf16[1200,512]{1,0:T(8,128)(2,1)}, bf16[1200,2048]{1,0:T(8,128)(2,1)}, /*index=5*/bf16[1200,2048]{1,0:T(8,128)(2,1)}) custom-call(bf16[6,196,512]{2,1,0:T(8,128)(2,1)} %constant_dynamic-slice_fusion.2.x_ref, bf16[2,512,3072]{2,1,0:T(8,128)(2,1)} %bitcast.154, ...), custom_call_target="tpu_custom_call" | custom-call | tf_op jit(solution)/shard_map/forward_0/pallas_call | solution.py:342
  133.4 42.4 %forward_1.1 = (f32[6,196,512]{2,1,0:T(8,128)}, f32[1200,512]{1,0:T(8,128)}, bf16[1536,1536]{1,0:T(8,128)(2,1)}, bf16[1200,512]{1,0:T(8,128)(2,1)}, bf16[1200,20...) custom-call(f32[1200,512]{1,0:T(8,128)} %get-tuple-element.57.x_ref, bf16[2,512,3072]{2,1,0:T(8,128)(2,1)} %bitcast.150, ...), custom_call_target="tpu_custom_call" | custom-call | tf_op jit(solution)/shard_map/forward_1/pallas_call | solution.py:342
  175.7 0.6 broadcast_in_dim.2.live_ref
  176.4 56.2 %backward_1.1 = (f32[1200,512]{1,0:T(8,128)}, bf16[2,512,3072]{2,1,0:T(8,128)(2,1)}, f32[2,512]{1,0:T(2,128)}, f32[1,2048]{1,0:T(1,128)}, f32[2,64,512]{2,1,0:T(8,128)}, /*index=5*/f32[8,512]{1,0:T(8,128)}) custom-call(f32[6,196,512]{2,1,0:T(8,128)} %constant_dynamic-slice_fusion.1.g_ref, f32[1200,512]{1,0:T(8,128)} %get-tuple-element.57.x_ref, ...), custom_call_target="tpu_custom_call" | custom-call | tf_op jit(solution)/shard_map/backward_1/pallas_call | solution.py:387
  232.7 56.2 %backward_0.1 = (f32[6,196,512]{2,1,0:T(8,128)}, bf16[2,512,3072]{2,1,0:T(8,128)(2,1)}, f32[2,512]{1,0:T(2,128)}, f32[1,2048]{1,0:T(1,128)}, f32[2,64,512]{2,1,0:T(8,128)}, /*index=5*/f32[8,512]{1,0:T(8,128)}) custom-call(f32[1200,512]{1,0:T(8,128)} %get-tuple-element.65.g_ref, bf16[6,196,512]{2,1,0:T(8,128)(2,1)} %constant_dynamic-slice_fusion.2.x_ref, ...), custom_call_target="tpu_custom_call" | custom-call | tf_op jit(solution)/shard_map/backward_0/pallas_call | solution.py:387
  289.6 1.1 copy.156
  291.0 0.9 fusion.6
  292.2 1.1 copy.157
  293.5 0.9 fusion.5
  295.6 59.7 %scatter_2.1 = (f32[32,3072]{1,0:T(8,128)}, f32[144,128]{1,0:T(8,128)}) custom-call(bf16[2,4,2,2,32,3072]{5,4,3,2,1,0:T(8,128)(2,1)} %bitcast.163, f32[144,128]{1,0:T(8,128)} %pad_bitcast_fusion.refs_0_), custom_call_target="tpu_custom_call" | custom-call | tf_op jit(solution)/shard_map/scatter_2/pallas_call | solution.py:820
  355.3 1.0 reshape.241
  356.3 0.7 slice.138
  357.0 48.4 %scatter_3.1 = f32[32,3072]{1,0:T(8,128)} custom-call(bf16[2,4,2,2,32,3072]{5,4,3,2,1,0:T(8,128)(2,1)} %bitcast.162), custom_call_target="tpu_custom_call" | custom-call | tf_op jit(solution)/shard_map/scatter_3/pallas_call | solution.py:820
  405.4 0.7 reshape.244
  406.2 0.9 multiply_subtract_fusion.7
  408.9 0.9 fusion.23
  409.8 1.4 multiply_subtract_fusion.6
  411.2 1.4 multiply_subtract_fusion.5
  412.6 1.5 multiply_subtract_fusion.4
  414.1 1.7 multiply_subtract_fusion.3
  415.8 0.9 multiply_subtract_fusion.2
  416.7 1.0 multiply_subtract_fusion
  417.7 1.0 multiply_subtract_fusion.1
  418.7 2.3 broadcast_select_fusion.1
  421.0 2.8 pad_maximum_fusion.1
  423.8 2.3 broadcast_select_fusion.3
  426.1 2.8 pad_maximum_fusion
  (112 shorter events, 8.2 us)
Async XLA Ops:
  0.7 83.1 %copy-start = (bf16[12,196,512]{2,1,0:T(8,128)(2,1)S(1)}, bf16[12,196,512]{2,1,0:T(8,128)(2,1)}, u32[]{:S(2)}) copy-start(bf16[12,196,512]{2,1,0:T(8,128)(2,1)} %param.34) | copy-start | bytes 7225348
  0.7 73.0 %copy-start.19 = (s32[49,49]{1,0:T(8,128)S(1)}, s32[49,49]{1,0:T(8,128)}, u32[]{:S(2)}) copy-start(s32[49,49]{1,0:T(8,128)} %param.37) | copy-start | bytes 28816
  72.0 5.5 %copy-start.18 = (f32[2,6,512]{2,0,1:T(2,128)S(1)}, f32[2,6,512]{2,0,1:T(2,128)}, u32[]{:S(2)}) copy-start(f32[2,6,512]{2,0,1:T(2,128)} %param.45) | copy-start | bytes 73732
  84.9 4.8 %copy-start.6 = (f32[4,64,512]{2,1,0:T(8,128)S(1)}, f32[4,64,512]{2,1,0:T(8,128)}, u32[]{:S(2)}) copy-start(f32[4,64,512]{2,1,0:T(8,128)} %add.179) | copy-start | bytes 1572868
  84.9 4.8 %copy-start.7 = (f32[2,64,512]{2,1,0:T(8,128)S(1)}, f32[2,64,512]{2,1,0:T(8,128)}, u32[]{:S(2)}) copy-start(f32[2,64,512]{2,1,0:T(8,128)} %add.176) | copy-start | bytes 786436
  232.6 56.7 %copy-start.4 = (f32[6,196,512]{2,1,0:T(8,128)S(1)}, f32[6,196,512]{2,1,0:T(8,128)}, u32[]{:S(2)}) copy-start(f32[6,196,512]{2,1,0:T(8,128)} %get-tuple-element.59) | copy-start | bytes 7225348
  232.7 56.8 %copy-start.20 = (s32[49,49]{1,0:T(8,128)S(1)}, s32[49,49]{1,0:T(8,128)}, u32[]{:S(2)}) copy-start(s32[49,49]{1,0:T(8,128)} %param.37) | copy-start | bytes 28816
  288.8 3.2 copy-start.22
  288.9 3.2 copy-start.26
  288.9 3.2 copy-start.24
  288.9 129.9 %collective-permute-start.1 = (f32[6,196,512]{2,1,0:T(8,128)}, f32[6,196,512]{2,1,0:T(8,128)}, u32[]{:S(2)}, u32[]{:S(2)}) collective-permute-start(f32[6,196,512]{2,1,0:T(8,128)} %get-tuple-element.71), channel_id=1, source_target_pairs={{0,1},{1,0},{2,3},{3,2},{4,5},{5,4},{6,7},{7,6},{8,9},{9,8},{10,11... | collective-permute-start | bytes 7225352 | tf_op jit(solution)/shard_map/ppermute | solution.py:841
  289.3 134.5 %collective-permute-start = (f32[6,196,512]{2,1,0:T(8,128)S(1)}, f32[6,196,512]{2,1,0:T(8,128)}, u32[]{:S(2)}, u32[]{:S(2)}) collective-permute-start(f32[6,196,512]{2,1,0:T(8,128)S(1)} %copy-done.4), channel_id=1, source_target_pairs={{0,1},{1,0},{2,3},{3,2},{4,5},{5,4},{6,7},{7,6},{8,9},{9,8},{10,11... | collective-permute-start | bytes 7225352 | tf_op jit(solution)/shard_map/ppermute | solution.py:841
  290.7 3.8 copy-start.21
  290.7 3.8 copy-start.25
  290.8 3.8 copy-start.23
  356.3 0.7 copy-start.11
  357.0 48.4 %slice-start = ((f32[2,8848]{1,0:T(2,128)}), f32[2,2704]{1,0:T(2,128)S(1)}, s32[]{:S(2)}) async-start(f32[2,8848]{1,0:T(2,128)} %copy-done.11), calls=%async_computation | async-start | bytes 45056 | tf_op jit(solution)/shard_map/slice | solution.py:942
  357.0 49.1 %slice-start.2 = ((f32[2,8848]{1,0:T(2,128)}), f32[2,1024]{1,0:T(2,128)S(1)}, s32[]{:S(2)}) async-start(f32[2,8848]{1,0:T(2,128)} %copy-done.11), calls=%async_computation.2 | async-start | bytes 16384 | tf_op jit(solution)/shard_map/slice | solution.py:939
  357.0 51.9 %copy-start.3 = (f32[32,3072]{1,0:T(8,128)S(1)}, f32[32,3072]{1,0:T(8,128)}, u32[]{:S(2)}) copy-start(f32[32,3072]{1,0:T(8,128)} %get-tuple-element.81) | copy-start | bytes 1179652
  357.0 52.8 %slice-start.1 = ((f32[2,8848]{1,0:T(2,128)}), f32[2,2048]{1,0:T(2,128)S(1)}, s32[]{:S(2)}) async-start(f32[2,8848]{1,0:T(2,128)} %copy-done.11), calls=%async_computation.1 | async-start | bytes 32768 | tf_op jit(solution)/shard_map/slice | solution.py:940
  405.4 11.3 %copy-start.2 = (f32[32,3072]{1,0:T(8,128)S(1)}, f32[32,3072]{1,0:T(8,128)}, u32[]{:S(2)}) copy-start(f32[32,3072]{1,0:T(8,128)} %scatter_3.1) | copy-start | bytes 1179652
  405.4 11.3 %copy-start.8 = (f32[2,1024,32]{1,2,0:T(8,128)S(1)}, f32[2,1024,32]{1,2,0:T(8,128)}, u32[]{:S(2)}) copy-start(f32[2,1024,32]{1,2,0:T(8,128)} %param.41) | copy-start | bytes 786436
  406.1 9.6 %copy-start.10 = (f32[2,32,3,256]{3,1,2,0:T(8,128)S(1)}, f32[2,32,3,256]{3,1,2,0:T(8,128)}, u32[]{:S(2)}) copy-start(f32[2,32,3,256]{3,1,2,0:T(8,128)} %param.38) | copy-start | bytes 589828
  406.2 9.6 %copy-start.16 = (f32[2,32,3,256]{3,1,2,0:T(8,128)S(1)}, f32[2,32,3,256]{3,1,2,0:T(8,128)}, u32[]{:S(2)}) copy-start(f32[2,32,3,256]{3,1,2,0:T(8,128)} %param.46) | copy-start | bytes 589828
  406.2 9.6 %copy-start.17 = (f32[2,32,3,256]{3,1,2,0:T(8,128)S(1)}, f32[2,32,3,256]{3,1,2,0:T(8,128)}, u32[]{:S(2)}) copy-start(f32[2,32,3,256]{3,1,2,0:T(8,128)} %param.54) | copy-start | bytes 589828
  406.2 10.5 %copy-start.12 = (f32[2,1024,32]{1,2,0:T(8,128)S(1)}, f32[2,1024,32]{1,2,0:T(8,128)}, u32[]{:S(2)}) copy-start(f32[2,1024,32]{1,2,0:T(8,128)} %param.49) | copy-start | bytes 786436
  406.2 10.5 %copy-start.13 = (f32[2,1024,32]{1,2,0:T(8,128)S(1)}, f32[2,1024,32]{1,2,0:T(8,128)}, u32[]{:S(2)}) copy-start(f32[2,1024,32]{1,2,0:T(8,128)} %param.57) | copy-start | bytes 786436
  414.1 3.6 copy-start.9
  414.1 3.6 copy-start.14
  414.1 3.7 copy-start.15
  416.7 2.0 copy-start.5
  426.1 2.8 copy-start.1

commit v3 on v2

--- a/solution.py
+++ b/solution.py
@@ -249,9 +249,18 @@
     return gmid + norm_back(gnorm, hat, inv, nv_ref[0:1, :])
 
 
-def forward_kernel(first, last, windows, x_ref, wm_ref, wa_ref, bias_ref, qvb_ref, b1_ref, nv_ref,
-                   perm_ref, perm_t_ref, hm_ref, y_ref, mid_ref, qkv_ref, mixed_ref, act_ref, slope_ref,
-                   xs, nperm, mixw):
+def forward_kernel(first, last, windows, carry, x_ref, wm_ref, wa_ref, bias_ref, qvb_ref, b1_ref, nv_ref,
+                   perm_ref, perm_t_ref, hm_ref, *refs):
+    i = pl.program_id(0)
+    if carry:
+        own_ref, y_ref, mid_ref, qkv_ref, mixed_ref, act_ref, slope_ref, full_ref = refs[:8]
+        xs, nperm, mixw, *sems = refs[8:]
+        comm = Gather(own_ref, full_ref, *sems, 0, COLS)
+        pl.when(i == 0)(lambda: neighbour_barrier(comm.p))
+    else:
+        y_ref, mid_ref, qkv_ref, mixed_ref, act_ref, slope_ref, xs, nperm, mixw = refs
+        comm = None
+    point(comm, i, 0)
     if first:
         put_images(xs, x_ref)
         x = xs[...]
@@ -260,22 +269,39 @@
     mid = attend_forward(x, wa_ref, bias_ref, qvb_ref, nv_ref, perm_ref, perm_t_ref, hm_ref,
                          qkv_ref, mixed_ref, nperm, mixw, windows)
     mid_ref[...] = mid
+    point(comm, i, 1)
     y = mlp_forward(mid, wm_ref, b1_ref, nv_ref, act_ref, slope_ref)
     if last:
         for im in range(PAIR):
             y_ref[im] = y[im * SEQP : im * SEQP + SEQ]
     else:
         y_ref[...] = y
+    if carry:
+        pl.when(i == 2)(lambda: comm.stage(6))
+
+
+def point(comm, i, at):
+    if comm is not None:
+        for step in range(3):
+            pl.when(i == step)(lambda step=step: comm.stage(2 * step + at))
 
 
 GW = 1024
 
 
-def backward_kernel(first, last, windows, steps, g_ref, x_ref, mid_ref, wm_ref, wa_ref, bias_ref, nv_ref,
-                    perm_ref, perm_t_ref, hm_ref, live_ref, qkv_ref, slope_ref, act_ref, mixed_ref,
-                    gx_ref, gw_ref, qv_acc, b1_acc, ds_acc, nv_acc,
-                    xs, gs, mperm, gmw, gqw, gp, gq_s, hid_s, gb_s, mb_s, nb_s):
+def backward_kernel(first, last, windows, steps, carry, g_ref, x_ref, mid_ref, wm_ref, wa_ref, bias_ref, nv_ref,
+                    perm_ref, perm_t_ref, hm_ref, live_ref, qkv_ref, slope_ref, act_ref, mixed_ref, *refs):
     i = pl.program_id(0)
+    if carry:
+        prev_ref, *refs = refs
+        sum_ref = refs.pop(6)
+        comm = Scatter(prev_ref, *refs[17:])
+        refs = refs[:17]
+        pl.when(i == 0)(lambda: neighbour_barrier(comm.p))
+    else:
+        comm = None
+    gx_ref, gw_ref, qv_acc, b1_acc, ds_acc, nv_acc, xs, gs, mperm, gmw, gqw, gp, gq_s, hid_s, gb_s, mb_s, nb_s = refs
+    point(comm, i, 0)
 
     @pl.when(i == 0)
     def _():
@@ -299,6 +325,7 @@
         else:
             x = x_ref[...]
         gmid = mlp_backward(gout, mid_ref[...], wm_ref, nv_ref, slope_ref, gp, hid_s, gb_s, rows, b1_acc, nv_acc)
+        point(comm, i, 1)
         gin = attend_backward(gmid, x, wa_ref, bias_ref, nv_ref, perm_ref, perm_t_ref, hm_ref, qkv_ref,
                               mperm, gmw, gqw, gq_s, mb_s, nb_s, rows, ds_acc, qv_acc, nv_acc, windows)
         if first:
@@ -307,6 +334,13 @@
         else:
             gx_ref[...] = gin
 
+    if carry:
+
+        @pl.when(i == steps)
+        def _():
+            comm.result(sum_ref)
+            comm.stage(6)
+
     for m in range(2):
 
         @pl.when(i == steps + 3 * m)
@@ -331,7 +365,7 @@
 VLIM = 60 * 1024 * 1024
 
 
-def forward_layer(layer, x, wg, bias, qvb, b1, nv, consts, steps):
+def forward_layer(layer, x, wg, bias, qvb, b1, nv, consts, steps, own=None):
     first, last = layer == 0, layer == LAYERS - 1
     shifted = layer % 2 == 1
     perm, perm_t, hm = consts
@@ -339,8 +373,21 @@
     windows = bias.shape[0]
     img = lambda: pl.BlockSpec((PAIR, SEQ, D), lambda i: (i, 0, 0))
     row = lambda n: pl.BlockSpec((ROWS, n), lambda i: (i, 0))
+    carry = own is not None
+    more = dict(in_specs=[], out_specs=[], out_shape=[], scratch=[], params={})
+    if carry:
+        more = dict(
+            in_specs=[whole(own.shape)],
+            out_specs=[pl.BlockSpec(memory_space=pl.ANY)],
+            out_shape=[jax.ShapeDtypeStruct((2, NZ, NY, NX, *own.shape), bf16)],
+            scratch=[
+                pltpu.SemaphoreType.DMA((Gather.SEMS,)), pltpu.SemaphoreType.DMA((Gather.SEMS,)),
+                pltpu.SemaphoreType.DMA((1,)),
+            ],
+            params=dict(collective_id=8 + layer, has_side_effects=True),
+        )
     return pl.pallas_call(
-        functools.partial(forward_kernel, first, last, windows),
+        functools.partial(forward_kernel, first, last, windows, carry),
         name=f"forward_{layer}",
         grid=(steps,),
         in_specs=[
@@ -349,11 +396,11 @@
             pl.BlockSpec((2, D, COLS - ATT), lambda i: (0, 0, ATT // (COLS - ATT)), pipeline_mode=pl.Buffered(1)),
             whole(bias.shape), whole(qvb.shape), whole(b1.shape), whole(nv.shape),
             whole(perm.shape), whole(perm_t.shape), whole(hm.shape),
-        ],
+        ] + more["in_specs"],
         out_specs=[
             img() if last else row(D), row(D),
             pl.BlockSpec((WPAIR, 2 * QKV), lambda i: (i, 0)), row(D), row(2 * FFH), row(2 * FFH),
-        ],
+        ] + more["out_specs"],
         out_shape=[
             jax.ShapeDtypeStruct((nimg, SEQ, D) if last else (nimg * SEQP, D), f32),
             jax.ShapeDtypeStruct((nimg * SEQP, D), f32),
@@ -361,15 +408,15 @@
             jax.ShapeDtypeStruct((nimg * SEQP, D), bf16),
             jax.ShapeDtypeStruct((nimg * SEQP, 2 * FFH), bf16),
             jax.ShapeDtypeStruct((nimg * SEQP, 2 * FFH), bf16),
-        ],
+        ] + more["out_shape"],
         scratch_shapes=[
             pltpu.VMEM((ROWS, D), f32), pltpu.VMEM((WPAIR, D), bf16), pltpu.VMEM((WPAIR, D), bf16),
-        ],
-        compiler_params=pltpu.CompilerParams(vmem_limit_bytes=VLIM),
-    )(x, wg, wg, bias, qvb, b1, nv, perm, perm_t, hm)
-
-
-def backward_layer(layer, grad, x, saved, wg, bias, nv, consts, live, steps):
+        ] + more["scratch"],
+        compiler_params=pltpu.CompilerParams(vmem_limit_bytes=VLIM, **more["params"]),
+    )(x, wg, wg, bias, qvb, b1, nv, perm, perm_t, hm, *([own] if carry else []))
+
+
+def backward_layer(layer, grad, x, saved, wg, bias, nv, consts, live, steps, prev=None):
     first, last = layer == 0, layer == LAYERS - 1
     perm, perm_t, hm = consts
     mid, qkv, mixed, act, slope = saved
@@ -384,8 +431,19 @@
         k = jnp.maximum(i - steps, 0)
         return (k // 3, 0, lax.rem(k, 3))
 
+    carry = prev is not None
+    more = dict(in_specs=[], out_specs=[], out_shape=[], scratch=[], params={})
+    if carry:
+        rows, cols = prev.shape[-2:]
+        more = dict(
+            in_specs=[pl.BlockSpec(memory_space=pl.ANY)],
+            out_specs=[whole((rows, cols))],
+            out_shape=[jax.ShapeDtypeStruct((rows, cols), f32)],
+            scratch=Scatter.scratch(rows, cols),
+            params=dict(collective_id=10 + layer, has_side_effects=True),
+        )
     return pl.pallas_call(
-        functools.partial(backward_kernel, first, last, windows, steps),
+        functools.partial(backward_kernel, first, last, windows, steps, carry),
         name=f"backward_{layer}",
         grid=(steps + 6,),
         in_specs=[
@@ -396,12 +454,12 @@
             pl.BlockSpec((None, PAIR, 128), lambda i: (jnp.minimum(i, top), 0, 0)),
             pl.BlockSpec((WPAIR, 2 * QKV), lambda i: (jnp.minimum(i, top), 0)), row(2 * FFH),
             whole(act.shape), whole(mixed.shape),
-        ],
+        ] + more["in_specs"],
         out_specs=[
             img() if first else row(D),
             pl.BlockSpec((1, D, GW), gmap),
             whole((2, 2 * HALF)), whole((1, 2 * FFH)), whole((2, WROW, LANES)), whole((8, D)),
-        ],
+        ] + more["out_specs"],
         out_shape=[
             jax.ShapeDtypeStruct((nimg, SEQ, D) if first else (total, D), f32),
             jax.ShapeDtypeStruct((2, D, COLS), bf16),
@@ -409,16 +467,16 @@
             jax.ShapeDtypeStruct((1, 2 * FFH), f32),
             jax.ShapeDtypeStruct((2, WROW, LANES), f32),
             jax.ShapeDtypeStruct((8, D), f32),
-        ],
+        ] + more["out_shape"],
         scratch_shapes=[
             pltpu.VMEM((ROWS, D), f32), pltpu.VMEM((ROWS, D), f32),
             pltpu.VMEM((WPAIR, D), bf16), pltpu.VMEM((WPAIR, D), bf16), pltpu.VMEM((WPAIR, 2 * QKV), bf16),
             pltpu.VMEM((total, 2 * FFH), bf16), pltpu.VMEM((total, 2 * QKV), bf16),
             pltpu.VMEM((total, D), bf16), pltpu.VMEM((total, D), bf16),
             pltpu.VMEM((total, D), bf16), pltpu.VMEM((total, D), bf16),
-        ],
-        compiler_params=pltpu.CompilerParams(vmem_limit_bytes=VLIM),
-    )(grad, x, mid, wg, wg, bias, nv, perm, perm_t, hm, live, qkv, slope, act, mixed)
+        ] + more["scratch"],
+        compiler_params=pltpu.CompilerParams(vmem_limit_bytes=VLIM, **more["params"]),
+    )(grad, x, mid, wg, wg, bias, nv, perm, perm_t, hm, live, qkv, slope, act, mixed, *([prev] if carry else []))
 
 
 def head_mask():
@@ -752,19 +810,14 @@
                 self.copy(k).wait_send()
 
 
-def gather_kernel(own_ref, small_ref, full_a, full_b, both_ref, send, recv, local, ssend, srecv):
+def gather_kernel(own_ref, small_ref, full_ref, both_ref, send, recv, local, ssend, srecv):
     p = Place()
     neighbour_barrier(p)
     swap = remote(small_ref, both_ref.at[p.m], ssend.at[0], srecv.at[0], p.core())
     swap.start()
-    cols = own_ref.shape[-1]
     parts = []
-    for layer, full in enumerate((full_a, full_b)):
-        for lo, hi in ((ATT, COLS), (0, ATT)):
-            n = len(parts)
-            if cols != COLS:
-                lo, hi = lo * cols // COLS, hi * cols // COLS
-            parts.append(Gather(own_ref.at[layer], full, send.at[n], recv.at[n], local.at[n], lo, hi))
+    for n, (lo, hi) in enumerate(((ATT, COLS), (0, ATT))):
+        parts.append(Gather(own_ref, full_ref, send.at[n], recv.at[n], local.at[n], lo, hi))
     for n in range(Gather.STAGES):
         for g in parts:
             g.stage(n)
@@ -773,18 +826,17 @@
 
 
 def gather_all(packed, small):
-    rows, cols = packed.shape[1:]
+    rows, cols = packed.shape
     full = jax.ShapeDtypeStruct((2, NZ, NY, NX, rows, cols), bf16)
-    n = 2 * LAYERS
     return pl.pallas_call(
         gather_kernel,
         name="gather",
-        out_shape=[full, full, jax.ShapeDtypeStruct((2, *small.shape), f32)],
+        out_shape=[full, jax.ShapeDtypeStruct((2, *small.shape), f32)],
         in_specs=[pl.BlockSpec(memory_space=pltpu.VMEM)] * 2,
-        out_specs=[pl.BlockSpec(memory_space=pl.ANY)] * 2 + [pl.BlockSpec(memory_space=pltpu.VMEM)],
+        out_specs=[pl.BlockSpec(memory_space=pl.ANY), pl.BlockSpec(memory_space=pltpu.VMEM)],
         scratch_shapes=[
-            pltpu.SemaphoreType.DMA((n, Gather.SEMS)), pltpu.SemaphoreType.DMA((n, Gather.SEMS)),
-            pltpu.SemaphoreType.DMA((n, 1)), pltpu.SemaphoreType.DMA((1,)), pltpu.SemaphoreType.DMA((1,)),
+            pltpu.SemaphoreType.DMA((2, Gather.SEMS)), pltpu.SemaphoreType.DMA((2, Gather.SEMS)),
+            pltpu.SemaphoreType.DMA((2, 1)), pltpu.SemaphoreType.DMA((1,)), pltpu.SemaphoreType.DMA((1,)),
         ],
         compiler_params=pltpu.CompilerParams(collective_id=1, has_side_effects=True),
     )(packed, small)
@@ -876,8 +928,8 @@
         [qv_bias.reshape(LAYERS, -1), fc_one_bias, rel_table.reshape(LAYERS, -1)], 1
     )
     if fast:
-        *weights, small = gather_all(packed, lanes_of(small))
-        weights = [w.reshape(2, D, COLS) for w in weights]
+        weights, small = gather_all(packed[0], lanes_of(small))
+        weights = [weights.reshape(2, D, COLS)]
         small = small.reshape(2, -1)[:, : LAYERS * SMALL].reshape(2, LAYERS, SMALL)
     else:
         weights = lax.all_gather(packed, ("mp", "dp")).reshape(2, -1, LAYERS, part, COLS)
@@ -901,24 +953,29 @@
         consts = (jnp.asarray(p, bf16), jnp.asarray(p.T, bf16), hm)
         ctx.append((wg, bias, consts))
         xs.append(x)
-        x, *kept = forward_layer(layer, x, wg, bias, qvb[:, layer], b1[layer], norm_vec[layer], consts, steps)
+        own = packed[layer + 1] if fast and layer + 1 < LAYERS else None
+        x, *kept = forward_layer(layer, x, wg, bias, qvb[:, layer], b1[layer], norm_vec[layer], consts, steps, own)
+        if own is not None:
+            weights.append(kept.pop().reshape(2, D, COLS))
         saved.append(kept)
     out = both_halves(x, me)
     g = cot
+    waiting = None
     big, little = [None] * LAYERS, [None] * LAYERS
     for layer in reversed(range(LAYERS)):
         wg, bias, consts = ctx[layer]
-        g, gw, gqv, gb1, ds, gnv = backward_layer(
-            layer, g, xs[layer], saved[layer], wg, bias, norm_vec[layer], consts, live, steps
+        g, gw, gqv, gb1, ds, gnv, *done = backward_layer(
+            layer, g, xs[layer], saved[layer], wg, bias, norm_vec[layer], consts, live, steps, waiting
         )
+        if done:
+            big[layer + 1] = done[0]
         ds = ds.reshape(2, WROW, GROUP, WROW)[:, :WSEQ, :, :WSEQ].transpose(0, 2, 3, 1)
         gt = jnp.dot(ds.reshape(2 * GROUP, WSEQ * WSEQ), onehot.T, precision=lax.Precision.HIGHEST)
         little[layer] = jnp.concatenate([gqv.reshape(-1), gb1.reshape(-1), gt.reshape(-1), gnv[:6].reshape(-1)])
         if fast:
             gw = gw.reshape(2, NZ, NY, NX, part, COLS)
-            if layer > 0:
-                (big[layer],) = scatter_sum(gw, None, 2 + layer)
-            else:
+            waiting = gw
+            if layer == 0:
                 big[layer], total = scatter_sum(gw, lanes_of(jnp.stack(little)), 2 + layer)
                 little = total.reshape(-1)[: LAYERS * LITTLE].reshape(LAYERS, LITTLE)
             continue

time: 436 us -> 397 us (0.911)
  Pallas kernels: 368 us -> 324 us
  local copies, waits for them, and re-layouts: 25.3 us -> 32.9 us
    pallas_call x2 -> x1, Pallas kernels: 108 us -> 63.2 us  [scatter_sum(): pl.pallas_call(functools.partial(scatter_kernel, with_small), name=f'scat...]
    pallas_call x2, Pallas kernels: 112 us -> 130 us  [backward_layer(): pl.pallas_call(functools.partial(backward_kernel, first, last, windows, s...]
    pallas_call x3, Pallas kernels: 147 us -> 131 us  [the longest x2 93.7 us: forward_layer(): pl.pallas_call(functools.partial(forward_kernel, first, last, windows, ca...]
  transfers between devices with their start and end apart: 2 -> 2, of which waited for: 0 -> 0; matrix products, arithmetic and copies ran while one was open for 6% -> 9% of each run, Pallas kernels for 25% -> 16%
where the time goes in v3:
time: 397 us; the launch traced here: 391 us
  Pallas kernels  324 us (82%)
  local copies, waits for them, and re-layouts  32.9 us (8%)
  other arithmetic  25.9 us (7%)
  matrix products  5.74 us (1%)
    pallas_call x2, Pallas kernels, backward_layer(): pl.pallas_call(functools.partial(backward_kernel, first, last, windows, s...  130 us
    pallas_call x2, Pallas kernels, forward_layer(): pl.pallas_call(functools.partial(forward_kernel, first, last, windows, ca...  93.7 us
    pallas_call x1, Pallas kernels, scatter_sum(): pl.pallas_call(functools.partial(scatter_kernel, with_small), name=f'scat...  63.2 us
    pallas_call x1, Pallas kernels, gather_all(): pl.pallas_call(gather_kernel, name='gather', out_shape=[full, jax.ShapeDt...  37 us
    sub x8, other arithmetic, adam_update(): weight_in - learn_rate * (hat_one / (jnp.sqrt(hat_two) + adam_eps) + deca...  9.59 us
  transfers between devices with their start and end apart: 2, of which 0 were waited for; matrix products, arithmetic and copies ran while one was open for 9% of the time, Pallas kernels for 16%

profile of v3, /device:TPU:0, one launch (start us, length us, event | category | flops | bytes accessed | tf_op | source)
XLA Modules:
  0.0 391.2 jit_solution(12043151075994670332)
XLA Ops:
  0.7 1.1 convert_bitcast_fusion.1
  1.8 1.0 convert.15
  2.8 1.0 convert_bitcast_fusion
  3.8 0.8 convert_bitcast_fusion.2
  4.7 0.8 slice_bitcast_fusion.2
  6.5 37.0 %gather.1 = (bf16[2,4,2,2,32,3072]{5,4,3,2,1,0:T(8,128)(2,1)}, f32[2,48,128]{2,1,0:T(8,128)}) custom-call(bf16[32,3072]{1,0:T(8,128)(2,1)} %get-tuple-element.219.own_ref, f32[48,128]{1,0:T(8,128)} %pad_bitcast_fusion.1.small_ref), custom_call_target="tpu_custom_call" | custom-call | tf_op jit(solution)/shard_map/gather/pallas_call | solution.py:831
  43.5 0.8 copy.194
  45.4 0.7 fusion.50
  46.2 2.0 fusion.9
  48.5 0.9 reshape_broadcast_in_dim.3.bias_ref
  50.0 1.0 copy.137
  51.0 2.0 fusion.12
  53.3 0.9 add.176
  54.2 1.0 add.178
  55.1 1.1 add.179
  56.2 1.2 constant_dynamic-slice_fusion.2.x_ref
  57.4 3.5 constant_dynamic-slice_fusion.1.g_ref
  62.2 1.1 broadcast_add_fusion.bias_ref
  63.3 51.4 %forward_0.1 = (f32[1200,512]{1,0:T(8,128)}, f32[1200,512]{1,0:T(8,128)}, bf16[1536,1536]{1,0:T(8,128)(2,1)}, bf16[1200,512]{1,0:T(8,128)(2,1)}, bf16[1200,2048]...) custom-call(bf16[6,196,512]{2,1,0:T(8,128)(2,1)} %constant_dynamic-slice_fusion.2.x_ref, ...), custom_call_target="tpu_custom_call" | custom-call | tf_op jit(solution)/shard_map/forward_0/pallas_call | solution.py:389
  114.7 42.3 %forward_1.1 = (f32[6,196,512]{2,1,0:T(8,128)}, f32[1200,512]{1,0:T(8,128)}, bf16[1536,1536]{1,0:T(8,128)(2,1)}, bf16[1200,512]{1,0:T(8,128)(2,1)}, bf16[1200,20...) custom-call(f32[1200,512]{1,0:T(8,128)} %get-tuple-element.58.x_ref, bf16[2,512,3072]{2,1,0:T(8,128)(2,1)} %bitcast.158, ...), custom_call_target="tpu_custom_call" | custom-call | tf_op jit(solution)/shard_map/forward_1/pallas_call | solution.py:389
  157.7 56.3 %backward_1.1 = (f32[1200,512]{1,0:T(8,128)}, bf16[2,512,3072]{2,1,0:T(8,128)(2,1)}, f32[2,512]{1,0:T(2,128)}, f32[1,2048]{1,0:T(1,128)}, f32[2,64,512]{2,1,0:T(8,128)}, /*index=5*/f32[8,512]{1,0:T(8,128)}) custom-call(f32[6,196,512]{2,1,0:T(8,128)} %constant_dynamic-slice_fusion.1.g_ref, f32[1200,512]{1,0:T(8,128)} %get-tuple-element.58.x_ref, ...), custom_call_target="tpu_custom_call" | custom-call | tf_op jit(solution)/shard_map/backward_1/pallas_call | solution.py:445
  214.0 73.6 %backward_0.1 = (f32[6,196,512]{2,1,0:T(8,128)}, bf16[2,512,3072]{2,1,0:T(8,128)(2,1)}, f32[2,512]{1,0:T(2,128)}, f32[1,2048]{1,0:T(1,128)}, f32[2,64,512]{2,1,0...) custom-call(f32[1200,512]{1,0:T(8,128)} %get-tuple-element.66.g_ref, ...), custom_call_target="tpu_custom_call" | custom-call | tf_op jit(solution)/shard_map/backward_0/pallas_call | solution.py:445
  288.3 1.1 copy.156
  289.7 0.9 fusion.6
  290.9 1.1 copy.157
  292.2 0.9 fusion.5
  294.9 63.2 %scatter_2.1 = (f32[32,3072]{1,0:T(8,128)}, f32[144,128]{1,0:T(8,128)}) custom-call(bf16[2,4,2,2,32,3072]{5,4,3,2,1,0:T(8,128)(2,1)} %bitcast.163, f32[144,128]{1,0:T(8,128)} %pad_bitcast_fusion.refs_0_), custom_call_target="tpu_custom_call" | custom-call | tf_op jit(solution)/shard_map/scatter_2/pallas_call | solution.py:872
  358.1 1.7 reshape.241
  359.8 1.3 slice.147
  361.2 0.8 slice.148
  362.0 1.3 slice.146
  363.3 1.3 slice.145
  364.6 1.5 reshape.244
  366.1 1.3 reshape.242
  367.4 0.8 constant_dynamic-slice_fusion
  368.2 0.8 multiply_subtract_fusion.7
  370.7 0.9 fusion.23
  371.7 1.4 multiply_subtract_fusion.6
  373.0 1.4 multiply_subtract_fusion.5
  374.4 1.5 multiply_subtract_fusion.4
  375.9 1.7 multiply_subtract_fusion.3
  377.6 0.9 multiply_subtract_fusion.2
  378.6 1.0 multiply_subtract_fusion
  379.6 1.0 multiply_subtract_fusion.1
  380.6 2.3 broadcast_select_fusion.1
  382.9 2.8 pad_maximum_fusion.1
  385.7 2.3 broadcast_select_fusion.3
  388.0 2.8 pad_maximum_fusion
  (111 shorter events, 9.6 us)
Async XLA Ops:
  0.7 55.5 %copy-start = (bf16[12,196,512]{2,1,0:T(8,128)(2,1)S(1)}, bf16[12,196,512]{2,1,0:T(8,128)(2,1)}, u32[]{:S(2)}) copy-start(bf16[12,196,512]{2,1,0:T(8,128)(2,1)} %param.34) | copy-start | bytes 7225348
  0.7 4.8 %copy-start.18 = (f32[2,169,8]{1,2,0:T(8,128)S(1)}, f32[2,169,8]{1,2,0:T(8,128)}, u32[]{:S(2)}) copy-start(f32[2,169,8]{1,2,0:T(8,128)} %param.44) | copy-start | bytes 32452
  0.7 5.0 %copy-start.24 = (f32[2,2,256]{2,1,0:T(2,128)S(1)}, f32[2,2,256]{2,1,0:T(2,128)}, u32[]{:S(2)}) copy-start(f32[2,2,256]{2,1,0:T(2,128)} %param.42) | copy-start | bytes 12292
  0.7 5.0 %copy-start.19 = (f32[2,1024]{1,0:T(2,128)S(1)}, f32[2,1024]{1,0:T(2,128)}, u32[]{:S(2)}) copy-start(f32[2,1024]{1,0:T(2,128)} %param.43) | copy-start | bytes 24580
  1.8 44.3 %copy-start.20 = (s32[49,49]{1,0:T(8,128)S(1)}, s32[49,49]{1,0:T(8,128)}, u32[]{:S(2)}) copy-start(s32[49,49]{1,0:T(8,128)} %param.37) | copy-start | bytes 28816
  44.5 5.5 %copy-start.17 = (f32[2,6,512]{2,0,1:T(2,128)S(1)}, f32[2,6,512]{2,0,1:T(2,128)}, u32[]{:S(2)}) copy-start(f32[2,6,512]{2,0,1:T(2,128)} %param.45) | copy-start | bytes 73732
  57.4 4.8 %copy-start.6 = (f32[4,64,512]{2,1,0:T(8,128)S(1)}, f32[4,64,512]{2,1,0:T(8,128)}, u32[]{:S(2)}) copy-start(f32[4,64,512]{2,1,0:T(8,128)} %add.179) | copy-start | bytes 1572868
  57.4 4.8 %copy-start.7 = (f32[2,64,512]{2,1,0:T(8,128)S(1)}, f32[2,64,512]{2,1,0:T(8,128)}, u32[]{:S(2)}) copy-start(f32[2,64,512]{2,1,0:T(8,128)} %add.176) | copy-start | bytes 786436
  214.0 73.7 %copy-start.4 = (f32[6,196,512]{2,1,0:T(8,128)S(1)}, f32[6,196,512]{2,1,0:T(8,128)}, u32[]{:S(2)}) copy-start(f32[6,196,512]{2,1,0:T(8,128)} %get-tuple-element.60) | copy-start | bytes 7225348
  214.0 74.2 %copy-start.21 = (s32[49,49]{1,0:T(8,128)S(1)}, s32[49,49]{1,0:T(8,128)}, u32[]{:S(2)}) copy-start(s32[49,49]{1,0:T(8,128)} %param.37) | copy-start | bytes 28816
  287.6 3.1 copy-start.23
  287.6 3.2 copy-start.27
  287.6 3.2 copy-start.26
  287.6 93.0 %collective-permute-start.1 = (f32[6,196,512]{2,1,0:T(8,128)}, f32[6,196,512]{2,1,0:T(8,128)}, u32[]{:S(2)}, u32[]{:S(2)}) collective-permute-start(f32[6,196,512]{2,1,0:T(8,128)} %get-tuple-element.73), channel_id=1, source_target_pairs={{0,1},{1,0},{2,3},{3,2},{4,5},{5,4},{6,7},{7,6},{8,9},{9,8},{10,11... | collective-permute-start | bytes 7225352 | tf_op jit(solution)/shard_map/ppermute | solution.py:893
  287.7 98.0 %collective-permute-start = (f32[6,196,512]{2,1,0:T(8,128)S(1)}, f32[6,196,512]{2,1,0:T(8,128)}, u32[]{:S(2)}, u32[]{:S(2)}) collective-permute-start(f32[6,196,512]{2,1,0:T(8,128)S(1)} %copy-done.4), channel_id=1, source_target_pairs={{0,1},{1,0},{2,3},{3,2},{4,5},{5,4},{6,7},{7,6},{8,9},{9,8},{10,11... | collective-permute-start | bytes 7225352 | tf_op jit(solution)/shard_map/ppermute | solution.py:893
  289.5 3.8 copy-start.22
  289.5 4.5 %copy-start.25 = (f32[1,2048]{1,0:T(1,128)S(1)}, f32[1,2048]{1,0:T(1,128)}, u32[]{:S(2)}) copy-start(f32[1,2048]{1,0:T(1,128)} %get-tuple-element.80) | copy-start | bytes 24580
  294.9 75.8 %copy-start.2 = (f32[32,3072]{1,0:T(8,128)S(1)}, f32[32,3072]{1,0:T(8,128)}, u32[]{:S(2)}) copy-start(f32[32,3072]{1,0:T(8,128)} %get-tuple-element.84) | copy-start | bytes 1179652
  358.1 20.4 %copy-start.3 = (f32[32,3072]{1,0:T(8,128)S(1)}, f32[32,3072]{1,0:T(8,128)}, u32[]{:S(2)}) copy-start(f32[32,3072]{1,0:T(8,128)} %get-tuple-element.83) | copy-start | bytes 1179652
  358.1 20.4 %copy-start.8 = (f32[2,1024,32]{1,2,0:T(8,128)S(1)}, f32[2,1024,32]{1,2,0:T(8,128)}, u32[]{:S(2)}) copy-start(f32[2,1024,32]{1,2,0:T(8,128)} %param.41) | copy-start | bytes 786436
  367.4 10.2 %copy-start.10 = (f32[2,32,3,256]{3,1,2,0:T(8,128)S(1)}, f32[2,32,3,256]{3,1,2,0:T(8,128)}, u32[]{:S(2)}) copy-start(f32[2,32,3,256]{3,1,2,0:T(8,128)} %param.38) | copy-start | bytes 589828
  367.4 10.2 %copy-start.15 = (f32[2,32,3,256]{3,1,2,0:T(8,128)S(1)}, f32[2,32,3,256]{3,1,2,0:T(8,128)}, u32[]{:S(2)}) copy-start(f32[2,32,3,256]{3,1,2,0:T(8,128)} %param.46) | copy-start | bytes 589828
  367.4 10.2 %copy-start.16 = (f32[2,32,3,256]{3,1,2,0:T(8,128)S(1)}, f32[2,32,3,256]{3,1,2,0:T(8,128)}, u32[]{:S(2)}) copy-start(f32[2,32,3,256]{3,1,2,0:T(8,128)} %param.54) | copy-start | bytes 589828
  367.4 11.1 %copy-start.11 = (f32[2,1024,32]{1,2,0:T(8,128)S(1)}, f32[2,1024,32]{1,2,0:T(8,128)}, u32[]{:S(2)}) copy-start(f32[2,1024,32]{1,2,0:T(8,128)} %param.49) | copy-start | bytes 786436
  367.4 11.1 %copy-start.12 = (f32[2,1024,32]{1,2,0:T(8,128)S(1)}, f32[2,1024,32]{1,2,0:T(8,128)}, u32[]{:S(2)}) copy-start(f32[2,1024,32]{1,2,0:T(8,128)} %param.57) | copy-start | bytes 786436
  375.9 3.6 copy-start.9
  375.9 3.6 copy-start.13
  375.9 3.6 copy-start.14
  378.5 2.0 copy-start.5
  387.9 2.8 copy-start.1
